TPU v7x, 32 devices: a whole 2x2x4 slice. The times are simulated.
32 devices in a mesh: dp: 8 (over z, x), tensor: 4 (over y, core).
Axes of the slice: x: 2, y: 2, z: 4, core: 2. Of those that a mesh axis runs over, the one named last changes fastest.
Arguments:
- tokens: bfloat16 [16384, 768], P(('dp', 'tensor')), may hold values from -6 to 6
- gain_one: float32 [768], P('dp'), may hold values from 0.5 to 1.5
- gain_two: float32 [768], P('dp'), may hold values from 0.5 to 1.5
- qkv_weight: float32 [3, 768, 768], P(None, 'dp', 'tensor'), may hold values from -0.21875 to 0.21875
- feature_weight: float32 [12, 64, 64], P('tensor', 'dp'), may hold values from -1.5 to 1.5
- out_weight: float32 [768, 768], P('tensor', 'dp'), may hold values from -1.75 to 1.75
- up_weight: float32 [768, 3072], P('dp', 'tensor'), may hold values from -0.21875 to 0.21875
- down_weight: float32 [3072, 768], P('tensor', 'dp'), may hold values from -0.109375 to 0.109375
- cotangent: bfloat16 [16384, 768], P(('dp', 'tensor')), may hold values from -6 to 6
Outputs:
- block_out: float32 [16384, 768], P(('dp', 'tensor'))
- tokens_grad: float32 [16384, 768], P(('dp', 'tensor'))
- gain_one_grad: float32 [768], P('dp')
- gain_two_grad: float32 [768], P('dp')
- qkv_weight_grad: float32 [3, 768, 768], P(None, 'dp', 'tensor')
- feature_weight_grad: float32 [12, 64, 64], P('tensor', 'dp')
- out_weight_grad: float32 [768, 768], P('tensor', 'dp')
- up_weight_grad: float32 [768, 3072], P('dp', 'tensor')
- down_weight_grad: float32 [3072, 768], P('tensor', 'dp')
All inputs are finite; a program needn't handle non-finite values.
Results may differ from a plain program's by a relative error of at most 0.017.
Values may be sent and summed in bfloat16 or wider, within the bound.
A program may use at most 192 MiB of HBM per device.

v0:
```python
import jax
import jax.numpy as jnp
from jax import lax
from jax.sharding import PartitionSpec as P

GROUP = 64


highest = lax.Precision.HIGHEST
epsilon = 1e-05


def layer_norm(activations, gain_vector):
    center = activations - jnp.mean(activations, axis=-1, keepdims=True)
    spread = jnp.mean(center * center, axis=-1, keepdims=True)
    return center * lax.rsqrt(spread + epsilon) * gain_vector


def feature_map(logits):
    return jnp.concatenate(
        [jax.nn.softmax(logits, axis=-1), jax.nn.softmax(-logits, axis=-1)], axis=-1
    )


def gelu_tanh(upper_part):
    return jax.nn.gelu(upper_part, approximate=True)


def causal_mask(block_size):
    row_index = lax.broadcasted_iota(jnp.int32, (block_size, block_size), 0)
    column_index = lax.broadcasted_iota(jnp.int32, (block_size, block_size), 1)
    return (column_index <= row_index).astype(jnp.float32)


def matmul(left, right):
    return jnp.dot(left, right, preferred_element_type=jnp.float32)


def inner_rows(left, right):
    return lax.dot_general(
        left, right, (((0,), (0,)), ((), ())), preferred_element_type=jnp.float32
    )


def times_transposed(left, right):
    return lax.dot_general(
        left, right, (((1,), (1,)), ((), ())), preferred_element_type=jnp.float32
    )


def later_sums(block_values):
    return jnp.flip(jnp.cumsum(jnp.flip(block_values, 0), axis=0), 0) - block_values


def per_device(
    tokens,
    gain_one,
    gain_two,
    qkv_weight,
    feature_weight,
    out_weight,
    up_weight,
    down_weight,
    cotangent,
):
    bfloat = jnp.bfloat16
    single = jnp.float32
    qkv_full, feature_full, out_full, gain_first, gain_second = (
        lax.all_gather(qkv_weight.astype(bfloat), "dp", axis=1, tiled=True),
        lax.all_gather(feature_weight.astype(bfloat), "dp", axis=1, tiled=True),
        lax.all_gather(out_weight.astype(bfloat), "dp", axis=1, tiled=True),
        lax.all_gather(gain_one.astype(bfloat), "dp", axis=0, tiled=True),
        lax.all_gather(gain_two.astype(bfloat), "dp", axis=0, tiled=True),
    )
    up_full, down_full = (
        lax.all_gather(up_weight.astype(bfloat), "dp", axis=0, tiled=True),
        lax.all_gather(down_weight.astype(bfloat), "dp", axis=1, tiled=True),
    )
    token_values = tokens.astype(single)
    gain_first_values = gain_first.astype(single)
    gain_second_values = gain_second.astype(single)
    normed = layer_norm(token_values, gain_first_values).astype(bfloat)
    normed_full = lax.all_gather(normed, "tensor", axis=0, tiled=True)
    sequence = normed_full.shape[0]
    head_count = feature_full.shape[0]
    head_size = feature_full.shape[1]
    local_width = head_count * head_size
    blocks = sequence // GROUP
    projected = jnp.einsum("ld,cde->cle", normed_full, qkv_full, preferred_element_type=single)
    query_rows = projected[0].reshape(sequence, head_count, head_size)
    key_rows = projected[1].reshape(sequence, head_count, head_size)
    value_low = projected[2].astype(bfloat)
    feature_values = feature_full.astype(single)
    query_logits = jnp.einsum("lhd,hde->lhe", query_rows, feature_values, precision=highest)
    key_logits = jnp.einsum("lhd,hde->lhe", key_rows, feature_values, precision=highest)
    phi_query = feature_map(query_logits).astype(bfloat)
    phi_key = feature_map(key_logits).astype(bfloat)
    feature_count = phi_query.shape[-1]
    causal = causal_mask(GROUP)
    query_blocks = phi_query.reshape(blocks, GROUP, head_count, feature_count)
    key_blocks = phi_key.reshape(blocks, GROUP, head_count, feature_count)
    value_blocks = value_low.reshape(blocks, GROUP, head_count, head_size)
    query_single = query_blocks.astype(single)
    scores = (
        jnp.einsum("bqhf,bkhf->bhqk", query_blocks, key_blocks, preferred_element_type=single)
        * causal
    )
    score_low = scores.astype(bfloat)
    intra_num = jnp.einsum(
        "bhqk,bkhe->bqhe", score_low, value_blocks, preferred_element_type=single
    )
    intra_den = jnp.transpose(jnp.sum(score_low.astype(single), axis=-1), (0, 2, 1))
    states = jnp.einsum("bkhf,bkhe->bhfe", key_blocks, value_blocks, preferred_element_type=single)
    prefix_low = (jnp.cumsum(states, axis=0) - states).astype(bfloat)
    key_sums = jnp.sum(key_blocks.astype(single), axis=1)
    key_prefix = jnp.cumsum(key_sums, axis=0) - key_sums
    numerator = intra_num + jnp.einsum(
        "bqhf,bhfe->bqhe", query_blocks, prefix_low, preferred_element_type=single
    )
    denominator = intra_den + jnp.einsum(
        "bqhf,bhf->bqh", query_single, key_prefix, precision=highest
    )
    attended = (numerator / denominator[..., None]).reshape(sequence, local_width).astype(bfloat)
    middle = token_values + lax.psum_scatter(
        matmul(attended, out_full).astype(jnp.bfloat16), "tensor", scatter_dimension=0, tiled=True
    ).astype(jnp.float32)
    normed_two = layer_norm(middle, gain_second_values).astype(bfloat)
    normed_two_full = lax.all_gather(normed_two, "tensor", axis=0, tiled=True)
    upper_part = matmul(normed_two_full, up_full)
    hidden = gelu_tanh(upper_part).astype(bfloat)
    block_out = middle + lax.psum_scatter(
        matmul(hidden, down_full).astype(jnp.bfloat16), "tensor", scatter_dimension=0, tiled=True
    ).astype(jnp.float32)
    qkv_back, feature_back, out_back = (
        lax.all_gather(qkv_weight.astype(bfloat), "dp", axis=1, tiled=True),
        lax.all_gather(feature_weight.astype(bfloat), "dp", axis=1, tiled=True),
        lax.all_gather(out_weight.astype(bfloat), "dp", axis=1, tiled=True),
    )
    up_back, down_back = (
        lax.all_gather(up_weight.astype(bfloat), "dp", axis=0, tiled=True),
        lax.all_gather(down_weight.astype(bfloat), "dp", axis=1, tiled=True),
    )
    cotangent_full = lax.all_gather(cotangent, "tensor", axis=0, tiled=True)
    down_grad_local = inner_rows(hidden, cotangent_full)
    d_hidden = times_transposed(cotangent_full, down_back)
    gelu_pull = jax.vjp(gelu_tanh, upper_part)[1]
    d_upper = gelu_pull(d_hidden)[0].astype(bfloat)
    up_grad_local = inner_rows(normed_two_full, d_upper)
    d_normed_two = lax.psum_scatter(
        times_transposed(d_upper, up_back).astype(jnp.bfloat16),
        "tensor",
        scatter_dimension=0,
        tiled=True,
    ).astype(jnp.float32)
    second_pull = jax.vjp(layer_norm, middle, gain_second_values)[1]
    middle_part, gain_two_local = second_pull(d_normed_two)
    d_middle = cotangent.astype(single) + middle_part
    branch_grad_full = lax.all_gather(d_middle.astype(bfloat), "tensor", axis=0, tiled=True)
    out_grad_local = inner_rows(attended, branch_grad_full)
    d_attended = times_transposed(branch_grad_full, out_back).reshape(
        blocks, GROUP, head_count, head_size
    )
    d_numerator = (d_attended / denominator[..., None]).astype(bfloat)
    d_denominator = -jnp.sum(d_attended * numerator, axis=-1) / (denominator * denominator)
    d_scores = jnp.einsum(
        "bqhe,bkhe->bhqk", d_numerator, value_blocks, preferred_element_type=single
    )
    d_scores = d_scores + jnp.transpose(d_denominator, (0, 2, 1))[..., None]
    d_score_low = d_scores.astype(bfloat) * causal.astype(bfloat)
    d_prefix = jnp.einsum(
        "bqhf,bqhe->bhfe", query_blocks, d_numerator, preferred_element_type=single
    )
    d_states = later_sums(d_prefix).astype(bfloat)
    d_key_prefix = jnp.einsum("bqhf,bqh->bhf", query_single, d_denominator, precision=highest)
    d_key_sums = later_sums(d_key_prefix)
    d_phi_query = jnp.einsum(
        "bhqk,bkhf->bqhf", d_score_low, key_blocks, preferred_element_type=single
    )
    d_phi_query = d_phi_query + jnp.einsum(
        "bqhe,bhfe->bqhf", d_numerator, prefix_low, preferred_element_type=single
    )
    d_phi_query = d_phi_query + d_denominator[..., None] * key_prefix[:, None]
    d_phi_key = jnp.einsum(
        "bhqk,bqhf->bkhf", d_score_low, query_blocks, preferred_element_type=single
    )
    d_phi_key = d_phi_key + jnp.einsum(
        "bkhe,bhfe->bkhf", value_blocks, d_states, preferred_element_type=single
    )
    d_phi_key = d_phi_key + d_key_sums[:, None]
    d_value = jnp.einsum("bhqk,bqhe->bkhe", score_low, d_numerator, preferred_element_type=single)
    d_value = d_value + jnp.einsum(
        "bkhf,bhfe->bkhe", key_blocks, d_states, preferred_element_type=single
    )
    query_pull = jax.vjp(feature_map, query_logits)[1]
    key_pull = jax.vjp(feature_map, key_logits)[1]
    d_query_logits = query_pull(d_phi_query.reshape(sequence, head_count, feature_count))[0]
    d_key_logits = key_pull(d_phi_key.reshape(sequence, head_count, feature_count))[0]
    feature_back_values = feature_back.astype(single)
    feature_grad_local = jnp.einsum("lhd,lhe->hde", query_rows, d_query_logits, precision=highest)
    feature_grad_local = feature_grad_local + jnp.einsum(
        "lhd,lhe->hde", key_rows, d_key_logits, precision=highest
    )
    d_query = jnp.einsum(
        "lhe,hde->lhd", d_query_logits, feature_back_values, precision=highest
    ).reshape(sequence, local_width)
    d_key = jnp.einsum(
        "lhe,hde->lhd", d_key_logits, feature_back_values, precision=highest
    ).reshape(sequence, local_width)
    d_projected = jnp.stack([d_query, d_key, d_value.reshape(sequence, local_width)]).astype(bfloat)
    qkv_grad_local = jnp.einsum(
        "ld,cle->cde", normed_full, d_projected, preferred_element_type=single
    )
    d_normed = lax.psum_scatter(
        jnp.einsum("cle,cde->ld", d_projected, qkv_back, preferred_element_type=single).astype(
            jnp.bfloat16
        ),
        "tensor",
        scatter_dimension=0,
        tiled=True,
    ).astype(jnp.float32)
    first_pull = jax.vjp(layer_norm, token_values, gain_first_values)[1]
    token_part, gain_one_local = first_pull(d_normed)
    tokens_grad = d_middle + token_part
    (
        qkv_weight_grad,
        feature_weight_grad,
        out_weight_grad,
        up_weight_grad,
        down_weight_grad,
        gain_one_grad,
        gain_two_grad,
    ) = (
        lax.psum_scatter(qkv_grad_local, "dp", scatter_dimension=1, tiled=True),
        lax.psum_scatter(feature_grad_local, "dp", scatter_dimension=1, tiled=True),
        lax.psum_scatter(out_grad_local, "dp", scatter_dimension=1, tiled=True),
        lax.psum_scatter(up_grad_local, "dp", scatter_dimension=0, tiled=True),
        lax.psum_scatter(down_grad_local, "dp", scatter_dimension=1, tiled=True),
        lax.psum_scatter(gain_one_local, "dp", scatter_dimension=0, tiled=True),
        lax.psum_scatter(gain_two_local, "dp", scatter_dimension=0, tiled=True),
    )
    gain_one_grad, gain_two_grad = lax.psum((gain_one_grad, gain_two_grad), "tensor")
    return (
        block_out,
        tokens_grad,
        gain_one_grad,
        gain_two_grad,
        qkv_weight_grad,
        feature_weight_grad,
        out_weight_grad,
        up_weight_grad,
        down_weight_grad,
    )


def solution(mesh):
    return jax.shard_map(
        per_device,
        mesh=mesh,
        in_specs=(
            P(("dp", "tensor"), None),
            P("dp"),
            P("dp"),
            P(None, "dp", "tensor"),
            P("tensor", "dp", None),
            P("tensor", "dp"),
            P("dp", "tensor"),
            P("tensor", "dp"),
            P(("dp", "tensor"), None),
        ),
        out_specs=(
            P(("dp", "tensor"), None),
            P(("dp", "tensor"), None),
            P("dp"),
            P("dp"),
            P(None, "dp", "tensor"),
            P("tensor", "dp", None),
            P("tensor", "dp"),
            P("dp", "tensor"),
            P("tensor", "dp"),
        ),
        check_vma=False,
    )
```

profile of v0, /device:TPU:0, one launch (start us, length us, event | category | flops | bytes accessed | tf_op | source)
XLA Modules:
  0.0 908.6 jit_solution(13974600321885006443)
XLA Ops:
  14.7 23.1 %all-reduce.6 = (bf16[768]{0:T(1024)(128)(2,1)S(1)}, bf16[768]{0:T(1024)(128)(2,1)S(1)}) all-reduce(bf16[768]{0:T(1024)(128)(2,1)S(1)} %dynamic-update-slice, bf16[768]{0:T(1024)(128)(2,1)S(1)} %dynamic-update-slice.1), channel_id=1, replica_groups=mesh['dp'=8,'tensor'=4] {'dp'}, use_global_device_ids=true, to_apply=%add | all-reduce | flops 1536 | bytes 6144
  40.0 35.5 %all_gather.40 = bf16[3,768,192]{2,0,1:T(4,128)(2,1)S(1)} all-gather(bf16[3,96,192]{2,0,1:T(4,128)(2,1)S(1)} %copy.93), channel_id=1, replica_groups=mesh['dp'=8,'tensor'=4] {'dp'}, dimensions={1}, use_global_device_ids=true | all-gather | bytes 995328 | tf_op jit(solution)/shard_map/all_gather | solution.py:69
  77.6 26.0 %all_gather.41 = bf16[3,64,64]{2,1,0:T(8,128)(2,1)S(1)} all-gather(bf16[3,8,64]{2,1,0:T(8,128)(2,1)S(1)} %convert_element_type.142), channel_id=1, replica_groups=mesh['dp'=8,'tensor'=4] {'dp'}, dimensions={1}, use_global_device_ids=true | all-gather | bytes 27648 | tf_op jit(solution)/shard_map/all_gather | solution.py:70
  104.2 31.0 %all_gather.42 = bf16[192,768]{0,1:T(8,128)(2,1)S(1)} all-gather(bf16[192,96]{0,1:T(8,128)(2,1)S(1)} %copy.103), channel_id=1, replica_groups=mesh['dp'=8,'tensor'=4] {'dp'}, dimensions={1}, use_global_device_ids=true | all-gather | bytes 331776 | tf_op jit(solution)/shard_map/all_gather | solution.py:71
  211.7 33.2 %reduce-scatter.14.cloned.1.call-done = bf16[512,768]{1,0:T(8,128)(2,1)} async-done(((bf16[2048,768]{1,0:T(8,128)(2,1)}), bf16[512,768]{1,0:T(8,128)(2,1)}) %reduce-scatter.14.cloned.1.call-update) | async-done | bytes 786448 | tf_op jit(solution)/shard_map/reduce_scatter | solution.py:124
  251.5 28.2 %all-gather.15.cloned.1.call-done = bf16[2048,768]{1,0:T(8,128)(2,1)} async-done(((bf16[512,768]{1,0:T(8,128)(2,1)}), bf16[2048,768]{1,0:T(8,128)(2,1)}) %all-gather.15.cloned.1.call-update) | async-done | bytes 3145744 | tf_op jit(solution)/shard_map/all_gather | solution.py:143
  279.7 7.5 fusion.73
  287.2 36.6 %all-gather.11.cloned.1.call-done = bf16[768,768]{1,0:T(8,128)(2,1)} async-done(((bf16[96,768]{1,0:T(8,128)(2,1)}), bf16[768,768]{1,0:T(8,128)(2,1)}) %all-gather.11.cloned.1.call-update) | async-done | bytes 1179664 | tf_op jit(solution)/shard_map/all_gather | solution.py:76
  323.8 28.9 %all-gather.9.cloned.1.call-done = bf16[2048,768]{1,0:T(8,128)(2,1)} async-done(((bf16[512,768]{1,0:T(8,128)(2,1)}), bf16[2048,768]{1,0:T(8,128)(2,1)}) %all-gather.9.cloned.1.call-update) | async-done | bytes 3145744 | tf_op jit(solution)/shard_map/all_gather | solution.py:128
  352.7 11.2 %fusion.10 = (bf16[2048,768]{1,0:T(8,128)(2,1)S(1)}, f32[2048,768]{1,0:T(8,128)}) fusion(f32[2048,768]{1,0:T(8,128)} %fusion.73, bf16[2048,768]{1,0:T(8,128)(2,1)} %all-gather.9.cloned.1.call-done, bf16[768,768]{1,0:T(8,128)(2,1)} %all-gather.11.cloned.1.call-done), kind=kOutput, calls=%fused_computation.12 | convolution fusion | flops 2447376384 | bytes 20054016 | tf_op jit(solution)/shard_map/dot_general | solution.py:36
  369.7 8.7 convolution_convert_fusion.1
  378.9 28.9 %reduce-scatter.18.cloned.1.call-done = bf16[512,768]{1,0:T(8,128)(2,1)} async-done(((bf16[2048,768]{1,0:T(8,128)(2,1)}), bf16[512,768]{1,0:T(8,128)(2,1)}) %reduce-scatter.18.cloned.1.call-update) | async-done | bytes 786448 | tf_op jit(solution)/shard_map/reduce_scatter | solution.py:149
  410.9 37.1 %reduce-scatter.16.cloned.1.call-done = bf16[512,768]{1,0:T(8,128)(2,1)} async-done(((bf16[2048,768]{1,0:T(8,128)(2,1)}), bf16[512,768]{1,0:T(8,128)(2,1)}) %reduce-scatter.16.cloned.1.call-update) | async-done | bytes 786448 | tf_op jit(solution)/shard_map/reduce_scatter | solution.py:131
  454.1 28.2 %all-gather.17.cloned.1.call-done = bf16[2048,768]{1,0:T(8,128)(2,1)} async-done(((bf16[512,768]{1,0:T(8,128)(2,1)}), bf16[2048,768]{1,0:T(8,128)(2,1)}) %all-gather.17.cloned.1.call-update) | async-done | bytes 3145744 | tf_op jit(solution)/shard_map/all_gather | solution.py:158
  586.6 5.5 bitcast_convert_fusion
  592.1 6.9 fusion.79
  599.4 8.3 fusion.59
  616.2 36.5 %reduce-scatter.28.cloned.1.call-done = f32[96,576]{1,0:T(8,128)} async-done(((f32[768,576]{1,0:T(8,128)}), f32[96,576]{1,0:T(8,128)}) %reduce-scatter.28.cloned.1.call-update) | async-done | bytes 221200
  654.7 37.2 %reduce-scatter.20.cloned.1.call-done = bf16[512,768]{1,0:T(8,128)(2,1)} async-done(((bf16[2048,768]{1,0:T(8,128)(2,1)}), bf16[512,768]{1,0:T(8,128)(2,1)}) %reduce-scatter.20.cloned.1.call-update) | async-done | bytes 786448 | tf_op jit(solution)/shard_map/reduce_scatter | solution.py:213
  697.6 22.3 %all-reduce.4 = (f32[768]{0:T(1024)S(1)}, f32[768]{0:T(1024)S(1)}) all-reduce(f32[768]{0:T(1024)S(1)} %get-tuple-element.47, f32[768]{0:T(1024)S(1)} %copy-done.76), channel_id=6, replica_groups=mesh['dp'=8,'tensor'=4] {'dp'}, use_global_device_ids=true, to_apply=%region_32.33.clone | all-reduce | flops 1536 | bytes 12288
  720.1 6.5 all-reduce.5
  726.6 39.4 %reduce-scatter.24.cloned.1.call-done = f32[96,768]{1,0:T(8,128)} async-done(((f32[768,768]{1,0:T(8,128)}), f32[96,768]{1,0:T(8,128)}) %reduce-scatter.24.cloned.1.call-update) | async-done | bytes 294928 | tf_op jit(solution)/shard_map/reduce_scatter | solution.py:236
  766.0 73.0 %reduce-scatter.26.cloned.1.call-done = f32[768,96]{0,1:T(8,128)} async-done(((f32[768,768]{0,1:T(8,128)}), f32[768,96]{0,1:T(8,128)}) %reduce-scatter.26.cloned.1.call-update) | async-done | bytes 294928 | tf_op jit(solution)/shard_map/reduce_scatter | solution.py:237
  839.0 61.8 %reduce-scatter.22.cloned.1.call-done = f32[3,8,64]{2,1,0:T(8,128)} async-done(((f32[3,64,64]{2,1,0:T(8,128)}), f32[3,8,64]{2,1,0:T(8,128)}) %reduce-scatter.22.cloned.1.call-update) | async-done | bytes 6160 | tf_op jit(solution)/shard_map/reduce_scatter | solution.py:234
  (331 shorter events, 228.5 us)
Async XLA Ops:
  8.0 30.4 %copy-start = (bf16[512,768]{1,0:T(8,128)(2,1)S(1)}, bf16[512,768]{1,0:T(8,128)(2,1)}, u32[]{:S(2)}) copy-start(bf16[512,768]{1,0:T(8,128)(2,1)} %param.9) | copy-start | bytes 2359300
  8.0 127.2 %all-gather.7.cloned.1.call-start = ((), (), s32[]{:S(2)}) async-start(), calls=%async_computation.9 | async-start | bytes 3932160 | tf_op jit(solution)/shard_map/all_gather | solution.py:83
  10.8 29.0 %copy-start.59 = (f32[3,96,192]{2,1,0:T(8,128)S(1)}, f32[3,96,192]{2,1,0:T(8,128)}, u32[]{:S(2)}) copy-start(f32[3,96,192]{2,1,0:T(8,128)} %param.12) | copy-start | bytes 663556
  39.6 205.3 %reduce-scatter.14.cloned.1.call-start = ((), (), s32[]{:S(2)}) async-start(), calls=%async_computation.10 | async-start | bytes 3932160 | tf_op jit(solution)/shard_map/reduce_scatter | solution.py:124
  103.6 41.7 %copy-start.44 = (bf16[3,64,64]{2,1,0:T(8,128)(2,1)}, bf16[3,64,64]{2,1,0:T(8,128)(2,1)S(1)}, u32[]{:S(2)}) copy-start(bf16[3,64,64]{2,1,0:T(8,128)(2,1)S(1)} %all_gather.41) | copy-start | bytes 73732
  208.6 42.9 %all-gather.13.cloned.1.call-start = ((), (), s32[]{:S(2)}) async-start(), calls=%async_computation.13 | async-start | bytes 1327104 | tf_op jit(solution)/shard_map/all_gather | solution.py:77
  210.3 69.4 %all-gather.15.cloned.1.call-start = ((), (), s32[]{:S(2)}) async-start(), calls=%async_computation.15 | async-start | bytes 3932160 | tf_op jit(solution)/shard_map/all_gather | solution.py:143
  210.9 112.9 %all-gather.11.cloned.1.call-start = ((), (), s32[]{:S(2)}) async-start(), calls=%async_computation.12 | async-start | bytes 1327104 | tf_op jit(solution)/shard_map/all_gather | solution.py:76
  211.6 141.1 %all-gather.9.cloned.1.call-start = ((), (), s32[]{:S(2)}) async-start(), calls=%async_computation.11 | async-start | bytes 3932160 | tf_op jit(solution)/shard_map/all_gather | solution.py:128
  248.1 159.7 %reduce-scatter.18.cloned.1.call-start = ((), (), s32[]{:S(2)}) async-start(), calls=%async_computation.16 | async-start | bytes 3932160 | tf_op jit(solution)/shard_map/reduce_scatter | solution.py:149
  369.7 78.3 %reduce-scatter.16.cloned.1.call-start = ((), (), s32[]{:S(2)}) async-start(), calls=%async_computation.14 | async-start | bytes 3932160 | tf_op jit(solution)/shard_map/reduce_scatter | solution.py:131
  378.4 103.9 %all-gather.17.cloned.1.call-start = ((), (), s32[]{:S(2)}) async-start(), calls=%async_computation.17 | async-start | bytes 3932160 | tf_op jit(solution)/shard_map/all_gather | solution.py:158
  453.8 160.8 %reduce-scatter.30.cloned.1.call-start = ((), (), s32[]{:S(2)}) async-start(), calls=%async_computation.23 | async-start | bytes 884736
  506.3 146.4 %reduce-scatter.28.cloned.1.call-start = ((), (), s32[]{:S(2)}) async-start(), calls=%async_computation.22 | async-start | bytes 2211840
  585.2 106.7 %reduce-scatter.20.cloned.1.call-start = ((), (), s32[]{:S(2)}) async-start(), calls=%async_computation.18 | async-start | bytes 3932160 | tf_op jit(solution)/shard_map/reduce_scatter | solution.py:213
  592.1 173.9 %reduce-scatter.24.cloned.1.call-start = ((), (), s32[]{:S(2)}) async-start(), calls=%async_computation.20 | async-start | bytes 2654208 | tf_op jit(solution)/shard_map/reduce_scatter | solution.py:236
  599.1 239.9 %reduce-scatter.26.cloned.1.call-start = ((), (), s32[]{:S(2)}) async-start(), calls=%async_computation.21 | async-start | bytes 2654208 | tf_op jit(solution)/shard_map/reduce_scatter | solution.py:237
  607.8 293.0 %reduce-scatter.22.cloned.1.call-start = ((), (), s32[]{:S(2)}) async-start(), calls=%async_computation.19 | async-start | bytes 110592 | tf_op jit(solution)/shard_map/reduce_scatter | solution.py:234
  614.5 77.4 %copy-start.68 = (f32[768]{0:T(1024)S(1)}, f32[768]{0:T(1024)}, u32[]{:S(2)}) copy-start(f32[768]{0:T(1024)} %copy-done.67) | copy-start | bytes 9220
  614.5 77.4 %copy-start.71 = (f32[512]{0:T(512)S(1)}, f32[512]{0:T(512)}, u32[]{:S(2)}) copy-start(f32[512]{0:T(512)} %copy-done.70) | copy-start | bytes 6148
  614.5 79.0 %copy-start.75 = (f32[512]{0:T(512)S(1)}, f32[512]{0:T(512)}, u32[]{:S(2)}) copy-start(f32[512]{0:T(512)} %copy-done.74) | copy-start | bytes 6148
  614.5 79.1 %copy-start.73 = (f32[512]{0:T(512)S(1)}, f32[512]{0:T(512)}, u32[]{:S(2)}) copy-start(f32[512]{0:T(512)} %copy-done.72) | copy-start | bytes 6148
  654.7 41.0 %copy-start.22 = (f32[512,768]{1,0:T(8,128)S(1)}, f32[512,768]{1,0:T(8,128)}, u32[]{:S(2)}) copy-start(f32[512,768]{1,0:T(8,128)} %copy-done.21) | copy-start | bytes 4718596
  654.7 41.1 %copy-start.38 = (bf16[512,768]{1,0:T(8,128)(2,1)S(1)}, bf16[512,768]{1,0:T(8,128)(2,1)}, u32[]{:S(2)}) copy-start(bf16[512,768]{1,0:T(8,128)(2,1)} %param.17) | copy-start | bytes 2359300
  (73 other events, 315.2 us)
Sparse Core Ops, SparseCore 0:
  39.7 25.7 all-gather.6
  208.8 36.0 reduce-scatter.13
  369.8 37.8 reduce-scatter.17
  410.1 37.8 reduce-scatter.15
Sparse Core Ops, SparseCore 1:
  211.9 39.6 all-gather.12
  252.9 26.7 all-gather.14
  282.3 41.4 all-gather.10
  325.9 26.7 all-gather.8
  453.9 28.3 all-gather.16
  506.4 63.2 reduce-scatter.29
  585.3 67.4 reduce-scatter.27
  655.2 36.7 reduce-scatter.19
  695.8 70.1 reduce-scatter.23
  770.1 68.8 reduce-scatter.25
  842.7 58.1 reduce-scatter.21
where the time goes:
time: 916 us; the launch traced here: 909 us
  waiting for transfers between devices  473 us (52%)
  blocking collectives  144 us (16%)
  matrix products  102 us (11%)
  local copies, waits for them, and re-layouts  101 us (11%)
  other arithmetic  67.7 us (7%)
  between operations  18.5 us (2%)
    reduce_scatter x1, waiting for transfers between devices, per_device(): lax.psum_scatter(down_grad_local, 'dp', scatter_dimension=1, tiled=True)  73 us
    reduce_scatter x1, waiting for transfers between devices, per_device(): lax.psum_scatter(feature_grad_local, 'dp', scatter_dimension=1, tiled=True)  61.8 us
    unnamed x2, blocking collectives  45.4 us
    unnamed x181, local copies, waits for them, and re-layouts  41.3 us
    reduce_scatter x1, waiting for transfers between devices, per_device(): lax.psum_scatter(up_grad_local, 'dp', scatter_dimension=0, tiled=True)  39.4 us
    unnamed x17, waiting for transfers between devices  37.3 us
    reduce_scatter x1, waiting for transfers between devices, per_device(): lax.psum_scatter(jnp.einsum('cle,cde->ld', d_projected, qkv_back, preferr...  37.2 us
    reduce_scatter x1, waiting for transfers between devices, per_device(): lax.psum_scatter(matmul(hidden, down_full).astype(jnp.bfloat16), 'tensor'...  37.1 us
  transfers between devices with their start and end apart: 15, of which 13 were waited for; matrix products, arithmetic and copies ran while one was open for 15% of the time, Pallas kernels for 0%

commit v1 on v0

v1 whole, which is shorter than its diff:
```python
import functools

import jax
import jax.numpy as jnp
from jax import lax
from jax.experimental import pallas as pl
from jax.experimental.pallas import tpu as pltpu
from jax.sharding import PartitionSpec as P

bfloat = jnp.bfloat16
single = jnp.float32
EPSILON = 1e-5
HEAD = 64
FEAT = 128
LIMIT = 64000000


def mm(left, right):
    return jnp.dot(left, right, preferred_element_type=single)


def mm_tn(left, right):
    return lax.dot_general(left, right, (((0,), (0,)), ((), ())), preferred_element_type=single)


def mm_nt(left, right):
    return lax.dot_general(left, right, (((1,), (1,)), ((), ())), preferred_element_type=single)


def norm_parts(rows):
    center = rows - jnp.mean(rows, axis=-1, keepdims=True)
    spread = jnp.mean(center * center, axis=-1, keepdims=True)
    scale = lax.rsqrt(spread + EPSILON)
    return center * scale, scale


def norm_back(unit, scale, grad, gain):
    scaled = grad * gain
    return scale * (
        scaled
        - jnp.mean(scaled, axis=-1, keepdims=True)
        - unit * jnp.mean(scaled * unit, axis=-1, keepdims=True)
    )


def split_low(values):
    high = values.astype(bfloat)
    return high, (values - high.astype(single)).astype(bfloat)


def half_ones(width):
    row = lax.broadcasted_iota(jnp.int32, (width, width), 0) // HEAD
    column = lax.broadcasted_iota(jnp.int32, (width, width), 1) // HEAD
    return (row == column).astype(single).astype(bfloat)


def causal_keep(length):
    row = lax.broadcasted_iota(jnp.int32, (length, length), 0)
    column = lax.broadcasted_iota(jnp.int32, (length, length), 1)
    return column <= row


def features_kernel(x_ref, gain_ref, s_ref, f_ref, normed_ref, qk_ref, phi_ref, vx_ref, tot_ref):
    @pl.when(pl.program_id(0) == 0)
    def _():
        unit, _ = norm_parts(x_ref[...].astype(single))
        normed_ref[...] = (unit * gain_ref[...]).astype(bfloat)

    normed = normed_ref[...]
    heads = f_ref.shape[0]
    tokens = normed.shape[0]
    qk_width = heads * 2 * HEAD
    ones = half_ones(2 * FEAT)
    lane = lax.broadcasted_iota(jnp.int32, (1, HEAD), 1)
    tail = jnp.broadcast_to((lane < 2).astype(single).astype(bfloat), (tokens, HEAD))
    group = lax.broadcasted_iota(jnp.int32, (1, FEAT), 1) < HEAD
    value = mm(normed, s_ref[:, qk_width : qk_width + heads * HEAD]).astype(bfloat)
    for h in range(heads):
        pair = mm(normed, s_ref[:, h * FEAT : (h + 1) * FEAT])
        high, rest = split_low(pair)
        qk_ref[:, h * FEAT : (h + 1) * FEAT] = high
        logits = mm(high, f_ref[h]) + mm(rest, f_ref[h])
        sides = []
        for side in range(2):
            part = logits[:, side * FEAT : (side + 1) * FEAT]
            low_top = jnp.max(jnp.where(group, part, -jnp.inf), axis=-1, keepdims=True)
            high_top = jnp.max(jnp.where(group, -jnp.inf, part), axis=-1, keepdims=True)
            sides.append(jnp.exp(part - jnp.where(group, low_top, high_top)))
        raised = jnp.concatenate(sides, axis=-1)
        phi = (raised / mm(raised.astype(bfloat), ones)).astype(bfloat)
        phi_ref[:, h * 2 * FEAT : (h + 1) * 2 * FEAT] = phi
        extended = jnp.concatenate([value[:, h * HEAD : (h + 1) * HEAD], tail], axis=-1)
        vx_ref[:, h * FEAT : (h + 1) * FEAT] = extended
        tot_ref[h] = mm_tn(phi[:, FEAT:], extended).astype(bfloat)


def attend_kernel(
    x_ref, gain_ref, s_ref, phi_ref, vx_ref, state_ref, att_ref, inv_ref, middle_ref, normed_ref
):
    heads = state_ref.shape[0]
    tokens = x_ref.shape[0]
    keep = causal_keep(tokens)
    step = pl.program_id(0)

    @pl.when(step == 0)
    def _():
        middle_ref[...] = x_ref[...].astype(single)

    parts = []
    for h in range(heads):
        phi_q = phi_ref[:, h * 2 * FEAT : h * 2 * FEAT + FEAT]
        phi_k = phi_ref[:, h * 2 * FEAT + FEAT : (h + 1) * 2 * FEAT]
        scores = jnp.where(keep, mm_nt(phi_q, phi_k), 0.0).astype(bfloat)
        total = mm(scores, vx_ref[:, h * FEAT : (h + 1) * FEAT]) + mm(phi_q, state_ref[h])
        inverse = jnp.broadcast_to(1.0 / total[:, HEAD : HEAD + 1], (tokens, HEAD))
        inv_ref[0, :, h * HEAD : (h + 1) * HEAD] = inverse
        parts.append((total[:, :HEAD] * inverse).astype(bfloat))
    attended = jnp.concatenate(parts, axis=-1)
    att_ref[0] = attended
    base = heads * 3 * HEAD
    middle_ref[...] += mm_nt(attended, s_ref[:, base : base + heads * HEAD])

    @pl.when(step == pl.num_programs(0) - 1)
    def _():
        unit, _ = norm_parts(middle_ref[...])
        normed_ref[...] = (unit * gain_ref[...]).astype(bfloat)


def feed_kernel(
    middle_ref, gain_ref, normed_ref, cot_ref, u_ref, d_ref,
    out_ref, dmid_ref, branch_ref, gsum_ref, ug_ref, dg_ref, acc_ref,
):
    step = pl.program_id(0)
    normed = normed_ref[...]
    cot = cot_ref[...]
    upper = mm(normed, u_ref[...])
    square = upper * upper
    factor = 0.7978845608028654
    bent = jnp.tanh(factor * upper * (1.0 + 0.044715 * square))
    half = 0.5 * (1.0 + bent)
    hidden = (upper * half).astype(bfloat)
    slope = half + 0.5 * upper * (1.0 - bent * bent) * (
        factor * (1.0 + 3.0 * 0.044715 * square)
    )
    d_upper = (mm(cot, d_ref[...]) * slope).astype(bfloat)
    ug_ref[...] = mm_tn(normed, d_upper).astype(bfloat)
    dg_ref[...] = mm_tn(cot, hidden).astype(bfloat)
    more = mm_nt(hidden, d_ref[...])
    back = mm_nt(d_upper, u_ref[...])

    @pl.when(step == 0)
    def _():
        out_ref[...] = middle_ref[...] + more
        acc_ref[...] = back

    @pl.when(step > 0)
    def _():
        out_ref[...] += more
        acc_ref[...] += back

    @pl.when(step == pl.num_programs(0) - 1)
    def _():
        unit, scale = norm_parts(middle_ref[...])
        grad = acc_ref[...]
        gsum_ref[...] = jnp.sum(grad * unit, axis=0, keepdims=True)
        d_middle = cot.astype(single) + norm_back(unit, scale, grad, gain_ref[...])
        dmid_ref[...] = d_middle
        branch_ref[...] = d_middle.astype(bfloat)


def ratio_kernel(branch_ref, s_ref, att_ref, inv_ref, phi_ref, dn_ref, tot_ref):
    heads = tot_ref.shape[0]
    tokens = branch_ref.shape[0]
    base = heads * 3 * HEAD
    d_att = mm(branch_ref[...], s_ref[:, base : base + heads * HEAD])
    inverse = inv_ref[0]
    d_num = d_att * inverse
    against = d_num * att_ref[0].astype(single)
    lane = lax.broadcasted_iota(jnp.int32, (tokens, HEAD), 1)
    for h in range(heads):
        here = slice(h * HEAD, (h + 1) * HEAD)
        d_den = -jnp.sum(against[:, here], axis=-1, keepdims=True)
        high = d_den.astype(bfloat).astype(single)
        tail = jnp.where(lane == 0, high, jnp.where(lane == 1, d_den - high, 0.0))
        extended = jnp.concatenate([d_num[:, here], tail], axis=-1).astype(bfloat)
        dn_ref[:, h * FEAT : (h + 1) * FEAT] = extended
        tot_ref[h] = mm_tn(phi_ref[:, h * 2 * FEAT : h * 2 * FEAT + FEAT], extended).astype(bfloat)


def back_kernel(
    x_ref, gain_ref, normed_ref, dmid_ref, branch_ref, s_ref, f_ref, att_ref,
    qk_ref, phi_ref, vx_ref, dn_ref, state_ref, later_ref,
    tg_ref, gsum_ref, sg_ref, fg_ref, acc_ref,
):
    step = pl.program_id(0)
    heads = state_ref.shape[0]
    tokens = x_ref.shape[0]
    keep = causal_keep(tokens)
    ones = half_ones(2 * FEAT)
    pairs = []
    values = []
    for h in range(heads):
        phi_q = phi_ref[:, h * 2 * FEAT : h * 2 * FEAT + FEAT]
        phi_k = phi_ref[:, h * 2 * FEAT + FEAT : (h + 1) * 2 * FEAT]
        extended = vx_ref[:, h * FEAT : (h + 1) * FEAT]
        d_num = dn_ref[:, h * FEAT : (h + 1) * FEAT]
        scores = jnp.where(keep, mm_nt(phi_q, phi_k), 0.0).astype(bfloat)
        d_scores = jnp.where(keep, mm_nt(d_num, extended), 0.0).astype(bfloat)
        d_phi_q = mm(d_scores, phi_k) + mm_nt(d_num, state_ref[h])
        d_phi_k = mm_tn(d_scores, phi_q) + mm_nt(extended, later_ref[h])
        d_value = mm_tn(scores, d_num) + mm(phi_k, later_ref[h])
        values.append(d_value[:, :HEAD].astype(bfloat))
        d_phi = jnp.concatenate([d_phi_q, d_phi_k], axis=-1)
        phi = phi_ref[:, h * 2 * FEAT : (h + 1) * 2 * FEAT].astype(single)
        high, rest = split_low(d_phi * phi)
        mean = mm(high, ones) + mm(rest, ones)
        d_logits = (phi * (d_phi - mean)).astype(bfloat)
        pairs.append(mm_nt(d_logits, f_ref[h]).astype(bfloat))
        cross = mm_tn(qk_ref[:, h * FEAT : (h + 1) * FEAT], d_logits)
        fg_ref[h] = (
            cross[:HEAD, :HEAD]
            - cross[:HEAD, HEAD:FEAT]
            + cross[HEAD:, FEAT : FEAT + HEAD]
            - cross[HEAD:, FEAT + HEAD :]
        )
    projected = jnp.concatenate(pairs + values, axis=-1)
    width = heads * 3 * HEAD
    sg_ref[...] = jnp.concatenate(
        [mm_tn(normed_ref[...], projected), mm_tn(branch_ref[...], att_ref[0])], axis=-1
    ).astype(bfloat)
    more = mm_nt(projected, s_ref[:, :width])

    @pl.when(step == 0)
    def _():
        acc_ref[...] = more

    @pl.when(step > 0)
    def _():
        acc_ref[...] += more

    @pl.when(step == pl.num_programs(0) - 1)
    def _():
        unit, scale = norm_parts(x_ref[...].astype(single))
        grad = acc_ref[...]
        gsum_ref[...] = jnp.sum(grad * unit, axis=0, keepdims=True)
        tg_ref[...] = dmid_ref[...] + norm_back(unit, scale, grad, gain_ref[...])


def whole(array):
    return pl.BlockSpec(array.shape, lambda j: (0,) * len(array.shape))


def columns(array, groups):
    return pl.BlockSpec((array.shape[0], array.shape[1] // groups), lambda j: (0, j))


def leading(array, groups):
    rest = array.shape[1:]
    return pl.BlockSpec(
        (array.shape[0] // groups,) + rest, lambda j: (j,) + (0,) * len(rest)
    )


def stage(kernel, groups, inputs, outputs, scratch=()):
    kinds = {"w": lambda a, g: whole(a), "c": columns, "l": leading}
    return pl.pallas_call(
        kernel,
        grid=(groups,),
        in_specs=[kinds[kind](array, groups) for kind, array in inputs],
        out_specs=[
            kinds[kind](jax.ShapeDtypeStruct(shape, dtype), groups)
            for kind, shape, dtype in outputs
        ],
        out_shape=[jax.ShapeDtypeStruct(shape, dtype) for kind, shape, dtype in outputs],
        scratch_shapes=list(scratch),
        compiler_params=pltpu.CompilerParams(
            dimension_semantics=("arbitrary",), vmem_limit_bytes=LIMIT
        ),
    )(*[array for kind, array in inputs])


def state_before(totals, groups, later):
    every = lax.all_gather(totals, "tensor", axis=0)
    me = lax.axis_index("tensor")
    order = jnp.arange(groups)
    chosen = (order > me) if later else (order < me)
    shape = (groups,) + (1,) * totals.ndim
    return jnp.sum(
        jnp.where(chosen.reshape(shape), every.astype(single), 0.0), axis=0
    ).astype(bfloat)


def compute(groups, tokens, cotangent, gain_one, gain_two, feature, square, up, down):
    length, width = tokens.shape
    heads = feature.shape[0]
    zero = jnp.zeros_like(feature)
    top = jnp.concatenate([feature, -feature, zero, zero], axis=2)
    low = jnp.concatenate([zero, zero, feature, -feature], axis=2)
    maps = jnp.concatenate([top, low], axis=1)
    feat_all = heads * 2 * FEAT
    ext_all = heads * FEAT
    head_block = (groups, length, heads // groups * HEAD)
    normed, pair, phi, extended, totals = stage(
        features_kernel, groups,
        [("w", tokens), ("w", gain_one), ("c", square), ("l", maps)],
        [("w", (length, width), bfloat), ("c", (length, ext_all), bfloat),
         ("c", (length, feat_all), bfloat), ("c", (length, ext_all), bfloat),
         ("l", (heads, FEAT, FEAT), bfloat)],
    )
    before = state_before(totals, groups, False)
    attended, inverse, middle, normed_two = stage(
        attend_kernel, groups,
        [("w", tokens), ("w", gain_two), ("c", square), ("c", phi), ("c", extended), ("l", before)],
        [("l", head_block, bfloat), ("l", head_block, single),
         ("w", (length, width), single), ("w", (length, width), bfloat)],
    )
    block_out, d_middle, branch, gain_two_sum, up_grad, down_grad = stage(
        feed_kernel, groups,
        [("w", middle), ("w", gain_two), ("w", normed_two), ("w", cotangent), ("c", up), ("c", down)],
        [("w", (length, width), single), ("w", (length, width), single),
         ("w", (length, width), bfloat), ("w", (1, width), single),
         ("c", up.shape, bfloat), ("c", down.shape, bfloat)],
        [pltpu.VMEM((length, width), single)],
    )
    d_num, d_totals = stage(
        ratio_kernel, groups,
        [("w", branch), ("c", square), ("l", attended), ("l", inverse), ("c", phi)],
        [("c", (length, ext_all), bfloat), ("l", (heads, FEAT, FEAT), bfloat)],
    )
    after = state_before(d_totals, groups, True)
    tokens_grad, gain_one_sum, square_grad, feature_grad = stage(
        back_kernel, groups,
        [("w", tokens), ("w", gain_one), ("w", normed), ("w", d_middle), ("w", branch),
         ("c", square), ("l", maps), ("l", attended), ("c", pair), ("c", phi), ("c", extended),
         ("c", d_num), ("l", before), ("l", after)],
        [("w", (length, width), single), ("w", (1, width), single),
         ("c", square.shape, bfloat), ("l", feature.shape, single)],
        [pltpu.VMEM((length, width), single)],
    )
    return (
        block_out, tokens_grad, gain_one_sum, gain_two_sum,
        square_grad, feature_grad, up_grad, down_grad,
    )


def pack_square(qkv, out_weight):
    rows = qkv.shape[1]
    heads = qkv.shape[2] // HEAD
    query = qkv[0].reshape(rows, heads, 1, HEAD)
    key = qkv[1].reshape(rows, heads, 1, HEAD)
    pair = jnp.concatenate([query, key], axis=2).reshape(rows, heads * 2 * HEAD)
    return jnp.concatenate([pair, qkv[2], out_weight.T], axis=1)


def unpack_square(grad):
    rows, width = grad.shape
    part = width // 4
    heads = part // HEAD
    pair = grad[:, : 2 * part].reshape(rows, heads, 2, HEAD)
    query = pair[:, :, 0].reshape(rows, part)
    key = pair[:, :, 1].reshape(rows, part)
    return jnp.stack([query, key, grad[:, 2 * part : 3 * part]]), grad[:, 3 * part :].T


def per_device(
    groups, dp, tokens, gain_one, gain_two, qkv_weight, feature_weight, out_weight, up_weight,
    down_weight, cotangent,
):
    def gathered(block):
        rows = lax.all_gather(block, "dp", axis=0, tiled=True)
        return lax.all_gather(rows, "tensor", axis=1, tiled=True)

    def scattered(grad):
        rows = lax.psum_scatter(grad, "tensor", scatter_dimension=1, tiled=True)
        return lax.psum_scatter(rows, "dp", scatter_dimension=0, tiled=True).astype(single)

    square = gathered(pack_square(qkv_weight.astype(bfloat), out_weight.astype(bfloat)))
    up = gathered(up_weight.astype(bfloat))
    down = gathered(down_weight.astype(bfloat).T)
    feature = lax.all_gather(feature_weight.astype(bfloat), "dp", axis=1, tiled=True)
    feature = lax.all_gather(feature, "tensor", axis=0, tiled=True)
    gain_first = lax.all_gather(gain_one.astype(bfloat), "dp", axis=0, tiled=True)
    gain_second = lax.all_gather(gain_two.astype(bfloat), "dp", axis=0, tiled=True)
    (
        block_out, tokens_grad, gain_one_sum, gain_two_sum,
        square_grad, feature_grad, up_grad, down_grad,
    ) = compute(
        groups, tokens, cotangent, gain_first.astype(single)[None], gain_second.astype(single)[None],
        feature, square, up, down,
    )
    qkv_grad, out_grad = unpack_square(scattered(square_grad))
    up_out = scattered(up_grad)
    down_out = scattered(down_grad).T
    feature_out = lax.psum_scatter(feature_grad, "tensor", scatter_dimension=0, tiled=True)
    feature_out = lax.psum_scatter(feature_out, "dp", scatter_dimension=1, tiled=True)
    gains = lax.psum(jnp.concatenate([gain_one_sum[0], gain_two_sum[0]]), ("tensor", "dp"))
    rows = gain_one.shape[0]
    place = lax.axis_index("dp") * rows
    gain_one_out = lax.dynamic_slice(gains, (place,), (rows,))
    gain_two_out = lax.dynamic_slice(gains, (place + rows * dp,), (rows,))
    return (
        block_out, tokens_grad, gain_one_out, gain_two_out, qkv_grad, feature_out, out_grad,
        up_out, down_out,
    )


def solution(mesh):
    return jax.shard_map(
        functools.partial(per_device, mesh.shape["tensor"], mesh.shape["dp"]),
        mesh=mesh,
        in_specs=(
            P(("dp", "tensor"), None),
            P("dp"),
            P("dp"),
            P(None, "dp", "tensor"),
            P("tensor", "dp", None),
            P("tensor", "dp"),
            P("dp", "tensor"),
            P("tensor", "dp"),
            P(("dp", "tensor"), None),
        ),
        out_specs=(
            P(("dp", "tensor"), None),
            P(("dp", "tensor"), None),
            P("dp"),
            P("dp"),
            P(None, "dp", "tensor"),
            P("tensor", "dp", None),
            P("tensor", "dp"),
            P("dp", "tensor"),
            P("tensor", "dp"),
        ),
        check_vma=False,
    )
```

time: 916 us -> 780 us (0.85)
  matrix products: 102 us -> 0 us
  local copies, waits for them, and re-layouts: 101 us -> 5.34 us
  Pallas kernels: 0 us -> 94.8 us
  waiting for transfers between devices: 473 us -> 558 us
  blocking collectives: 144 us -> 90.1 us
  other arithmetic: 67.7 us -> 14.8 us
    dot_general x30 -> x0, matrix products: 95.9 us -> none  [the longest x3 22.6 us: matmul(): return jnp.dot(left, right, preferred_element_type=jnp.float32)]
    pallas_call x0 -> x5, Pallas kernels: none -> 94.8 us  [stage(): pl.pallas_call(kernel, grid=(groups,), in_specs=[kinds[kind](array, group...]
    all_gather x6 -> x8, waiting for transfers between devices: 125 us -> 197 us  [the longest x3 95.4 us: gathered(): rows = lax.all_gather(block, 'dp', axis=0, tiled=True)]
    all_gather x2 -> x1, blocking collectives: 66.6 us -> 5.58 us  [per_device(): feature = lax.all_gather(feature, 'tensor', axis=0, tiled=True)]
    reduce_scatter x7 -> x8, waiting for transfers between devices: 311 us -> 359 us  [the longest x3 182 us: scattered(): lax.psum_scatter(rows, 'dp', scatter_dimension=0, tiled=True).astype(single)]
    unnamed x181 -> x25, local copies, waits for them, and re-layouts: 41.3 us -> 1.91 us
    unnamed x17 -> x16, waiting for transfers between devices: 37.3 us -> 1.95 us
    psum x1, blocking collectives: 6.54 us -> 39.4 us  [per_device(): lax.psum(jnp.concatenate([gain_one_sum[0], gain_two_sum[0]]), ('tensor',...]
  transfers between devices with their start and end apart: 15 -> 16, of which waited for: 13 -> 14; matrix products, arithmetic and copies ran while one was open for 15% -> 2% of each run, Pallas kernels for 0% -> 7%
where the time goes in v1:
time: 780 us; the launch traced here: 779 us
  waiting for transfers between devices  558 us (72%)
  Pallas kernels  94.8 us (12%)
  blocking collectives  90.1 us (12%)
  between operations  14.9 us (2%)
  other arithmetic  14.8 us (2%)
    reduce_scatter x3, waiting for transfers between devices, scattered(): lax.psum_scatter(rows, 'dp', scatter_dimension=0, tiled=True).astype(single)  182 us
    reduce_scatter x3, waiting for transfers between devices, scattered(): rows = lax.psum_scatter(grad, 'tensor', scatter_dimension=1, tiled=True)  119 us
    all_gather x3, waiting for transfers between devices, gathered(): rows = lax.all_gather(block, 'dp', axis=0, tiled=True)  95.4 us
    pallas_call x5, Pallas kernels, stage(): pl.pallas_call(kernel, grid=(groups,), in_specs=[kinds[kind](array, group...  94.8 us
    all_gather x3, waiting for transfers between devices, gathered(): return lax.all_gather(rows, 'tensor', axis=1, tiled=True)  63.9 us
    reduce_scatter x1, waiting for transfers between devices, per_device(): lax.psum_scatter(feature_out, 'dp', scatter_dimension=1, tiled=True)  58.1 us
    psum x1, blocking collectives, per_device(): lax.psum(jnp.concatenate([gain_one_sum[0], gain_two_sum[0]]), ('tensor',...  39.4 us
    all_gather x2, waiting for transfers between devices, state_before(): every = lax.all_gather(totals, 'tensor', axis=0)  37.7 us
  transfers between devices with their start and end apart: 16, of which 14 were waited for; matrix products, arithmetic and copies ran while one was open for 2% of the time, Pallas kernels for 7%

profile of v1, /device:TPU:0, one launch (start us, length us, event | category | flops | bytes accessed | tf_op | source)
XLA Modules:
  0.0 779.3 jit_solution(10200828442833202097)
XLA Ops:
  9.7 44.9 %all-gather.11.cloned.1.call-done = bf16[768,768]{1,0:T(8,128)(2,1)} async-done(((bf16[96,768]{1,0:T(8,128)(2,1)}), bf16[768,768]{1,0:T(8,128)(2,1)}) %all-gather.11.cloned.1.call-update) | async-done | bytes 1179664 | tf_op jit(solution)/shard_map/all_gather | solution.py:370
  58.0 19.1 %all-reduce.2 = (bf16[768]{0:T(1024)(128)(2,1)S(1)}, bf16[768]{0:T(1024)(128)(2,1)S(1)}) all-reduce(bf16[768]{0:T(1024)(128)(2,1)S(1)} %dynamic-update-slice, bf16[768]{0:T(1024)(128)(2,1)S(1)} %dynamic-update-slice.1), channel_id=1, replica_groups=mesh['dp'=8,'tensor'=4] {'dp'}, use_global_device_ids=true, to_apply=%add | all-reduce | flops 1536 | bytes 6144
  77.7 26.0 %all_gather.46 = bf16[3,64,64]{2,1,0:T(8,128)(2,1)S(1)} all-gather(bf16[3,8,64]{2,1,0:T(8,128)(2,1)S(1)} %convert_element_type.46), channel_id=1, replica_groups=mesh['dp'=8,'tensor'=4] {'dp'}, dimensions={1}, use_global_device_ids=true | all-gather | bytes 27648 | tf_op jit(solution)/shard_map/all_gather | solution.py:380
  103.7 5.6 all_gather.47
  110.6 17.7 %shard_map.160 = (bf16[512,768]{1,0:T(8,128)(2,1)}, bf16[512,1536]{1,0:T(8,128)(2,1)}, bf16[512,3072]{1,0:T(8,128)(2,1)}, bf16[512,1536]{1,0:T(8,128)(2,1)}, bf16[12,128,128]{2,1,0:T(8,128)(2,1)}) custom-call(bf16[512,768]{1,0:T(8,128)(2,1)} %x_ref.5, f32[1,768]{1,0:T(1,128)} %reshape.37.gain_ref, bf16[768,3072]{1,0:T(8,128)(2,1)} %all-gather.13.cloned.1.call-done.s_ref, ...), custom_call_target="tpu_custom_call" | custom-call | tf_op jit(solution)/shard_map/pallas_call | solution.py:266
  128.4 7.9 %all-gather.15.cloned.1.call-done = bf16[768,768]{1,0:T(8,128)(2,1)} async-done(((bf16[96,768]{1,0:T(8,128)(2,1)}), bf16[768,768]{1,0:T(8,128)(2,1)}) %all-gather.15.cloned.1.call-update) | async-done | bytes 1179664 | tf_op jit(solution)/shard_map/all_gather | solution.py:370
  136.3 42.5 %all-gather.19.cloned.1.call-done = bf16[768,768]{1,0:T(8,128)(2,1)} async-done(((bf16[96,768]{1,0:T(8,128)(2,1)}), bf16[768,768]{1,0:T(8,128)(2,1)}) %all-gather.19.cloned.1.call-update) | async-done | bytes 1179664 | tf_op jit(solution)/shard_map/all_gather | solution.py:370
  179.7 19.5 %all-gather.23.cloned.1.call-done = bf16[48,128,128]{2,1,0:T(8,128)(2,1)} async-done(((bf16[12,128,128]{2,1,0:T(8,128)(2,1)}), bf16[48,128,128]{2,1,0:T(8,128)(2,1)}) %all-gather.23.cloned.1.call-update) | async-done | bytes 1572880 | tf_op jit(solution)/shard_map/all_gather | solution.py:283
  201.9 11.4 %shard_map.161 = (bf16[4,512,192]{2,1,0:T(8,128)(2,1)}, f32[4,512,192]{2,1,0:T(8,128)}, f32[512,768]{1,0:T(8,128)}, bf16[512,768]{1,0:T(8,128)(2,1)}) custom-call(bf16[512,768]{1,0:T(8,128)(2,1)} %x_ref.5, f32[1,768]{1,0:T(1,128)} %reshape.36.gain_ref, bf16[768,3072]{1,0:T(8,128)(2,1)} %all-gather.13.cloned.1.call-done.s_ref, ...), custom_call_target="tpu_custom_call" | custom-call | tf_op jit(solution)/shard_map/pallas_call | solution.py:266
  213.3 24.8 %all-gather.17.cloned.1.call-done.u_ref = bf16[768,3072]{1,0:T(8,128)(2,1)} async-done(((bf16[768,768]{1,0:T(8,128)(2,1)}), bf16[768,3072]{1,0:T(8,128)(2,1)}) %all-gather.17.cloned.1.call-update) | async-done | bytes 4718608 | tf_op jit(solution)/shard_map/all_gather | solution.py:371
  238.1 39.0 %all-gather.21.cloned.1.call-done.d_ref = bf16[768,3072]{1,0:T(8,128)(2,1)} async-done(((bf16[768,768]{1,0:T(8,128)(2,1)}), bf16[768,3072]{1,0:T(8,128)(2,1)}) %all-gather.21.cloned.1.call-update) | async-done | bytes 4718608 | tf_op jit(solution)/shard_map/all_gather | solution.py:371
  277.1 24.2 %shard_map.162 = (f32[512,768]{1,0:T(8,128)}, f32[512,768]{1,0:T(8,128)}, bf16[512,768]{1,0:T(8,128)(2,1)}, f32[1,768]{1,0:T(1,128)}, bf16[768,3072]{1,0:T(8,128)(2,1)}, /*index=5*/bf16[768,3072]{1,0:T(8,128)(2,1)}) custom-call(f32[512,768]{1,0:T(8,128)} %get-tuple-element.33.middle_ref, f32[1,768]{1,0:T(1,128)} %reshape.36.gain_ref, ...), custom_call_target="tpu_custom_call" | custom-call | tf_op jit(solution)/shard_map/pallas_call | solution.py:266
  301.3 13.4 %shard_map.163 = (bf16[512,1536]{1,0:T(8,128)(2,1)}, bf16[12,128,128]{2,1,0:T(8,128)(2,1)}) custom-call(bf16[512,768]{1,0:T(8,128)(2,1)} %get-tuple-element.38.branch_ref, bf16[768,3072]{1,0:T(8,128)(2,1)} %all-gather.13.cloned.1.call-done.s_ref, bf16[4,512,192]{2,1,0:T(8,128)(2,1)} %get-tuple-element.39.att_ref, f32[4,512,192]{2,1,0:T(8,128)} %get-tuple-element.41.inv_ref, ...), custom_call_target="tpu_custom_call" | custom-call | tf_op jit(solution)/shard_map/pallas_call | solution.py:266
  316.4 18.2 %all-gather.25.cloned.1.call-done = bf16[48,128,128]{2,1,0:T(8,128)(2,1)} async-done(((bf16[12,128,128]{2,1,0:T(8,128)(2,1)}), bf16[48,128,128]{2,1,0:T(8,128)(2,1)}) %all-gather.25.cloned.1.call-update) | async-done | bytes 1572880 | tf_op jit(solution)/shard_map/all_gather | solution.py:283
  334.6 2.7 fusion.later_ref
  337.2 28.2 %shard_map.164 = (f32[512,768]{1,0:T(8,128)}, f32[1,768]{1,0:T(1,128)}, bf16[768,3072]{1,0:T(8,128)(2,1)}, f32[12,64,64]{2,1,0:T(8,128)}) custom-call(bf16[512,768]{1,0:T(8,128)(2,1)} %x_ref.5, f32[1,768]{1,0:T(1,128)} %reshape.37.gain_ref, bf16[512,768]{1,0:T(8,128)(2,1)} %get-tuple-element.36.normed_ref, f32[512,768]{1,0:T(8,128)} %get-tuple-element.37.dmid_ref, ...), custom_call_target="tpu_custom_call" | custom-call | tf_op jit(solution)/shard_map/pallas_call | solution.py:266
  366.0 18.9 %reduce-scatter.21.cloned.1.call-done = bf16[768,768]{1,0:T(8,128)(2,1)} async-done(((bf16[768,3072]{1,0:T(8,128)(2,1)}), bf16[768,768]{1,0:T(8,128)(2,1)}) %reduce-scatter.21.cloned.1.call-update) | async-done | bytes 1179664 | tf_op jit(solution)/shard_map/reduce_scatter | solution.py:374
  385.0 50.1 %reduce-scatter.17.cloned.1.call-done = bf16[768,768]{1,0:T(8,128)(2,1)} async-done(((bf16[768,3072]{1,0:T(8,128)(2,1)}), bf16[768,768]{1,0:T(8,128)(2,1)}) %reduce-scatter.17.cloned.1.call-update) | async-done | bytes 1179664 | tf_op jit(solution)/shard_map/reduce_scatter | solution.py:374
  435.2 50.3 %reduce-scatter.9.cloned.1.call-done = bf16[768,768]{1,0:T(8,128)(2,1)} async-done(((bf16[768,3072]{1,0:T(8,128)(2,1)}), bf16[768,768]{1,0:T(8,128)(2,1)}) %reduce-scatter.9.cloned.1.call-update) | async-done | bytes 1179664 | tf_op jit(solution)/shard_map/reduce_scatter | solution.py:374
  485.7 39.4 %psum.7 = f32[1536]{0:T(1024)S(1)} all-reduce(f32[1536]{0:T(1024)S(1)} %pad_maximum_fusion.3), channel_id=1, replica_groups=mesh['dp'=8,'tensor'=4] {'tensor','dp'}, use_global_device_ids=true, to_apply=%region_2.3 | all-reduce | flops 1536 | bytes 12288 | tf_op jit(solution)/shard_map/psum | solution.py:396
  525.7 51.3 %reduce-scatter.23.cloned.1.call-done = bf16[96,768]{1,0:T(8,128)(2,1)} async-done(((bf16[768,768]{1,0:T(8,128)(2,1)}), bf16[96,768]{1,0:T(8,128)(2,1)}) %reduce-scatter.23.cloned.1.call-update) | async-done | bytes 147472 | tf_op jit(solution)/shard_map/reduce_scatter | solution.py:375
  578.6 65.3 %reduce-scatter.19.cloned.1.call-done = bf16[96,768]{1,0:T(8,128)(2,1)} async-done(((bf16[768,768]{1,0:T(8,128)(2,1)}), bf16[96,768]{1,0:T(8,128)(2,1)}) %reduce-scatter.19.cloned.1.call-update) | async-done | bytes 147472 | tf_op jit(solution)/shard_map/reduce_scatter | solution.py:375
  645.6 65.3 %reduce-scatter.11.cloned.1.call-done = bf16[96,768]{1,0:T(8,128)(2,1)} async-done(((bf16[768,768]{1,0:T(8,128)(2,1)}), bf16[96,768]{1,0:T(8,128)(2,1)}) %reduce-scatter.11.cloned.1.call-update) | async-done | bytes 147472 | tf_op jit(solution)/shard_map/reduce_scatter | solution.py:375
  714.7 58.1 %reduce-scatter.15.cloned.1.call-done = f32[3,8,64]{2,1,0:T(8,128)} async-done(((f32[3,64,64]{2,1,0:T(8,128)}), f32[3,8,64]{2,1,0:T(8,128)}) %reduce-scatter.15.cloned.1.call-update) | async-done | bytes 6160 | tf_op jit(solution)/shard_map/reduce_scatter | solution.py:395
  (94 shorter events, 20.5 us)
Async XLA Ops:
  7.2 47.5 %copy-start = (f32[96,768]{1,0:T(8,128)S(1)}, f32[96,768]{1,0:T(8,128)}, u32[]{:S(2)}) copy-start(f32[96,768]{1,0:T(8,128)} %param.15) | copy-start | bytes 884740
  7.2 47.4 %all-gather.11.cloned.1.call-start = ((), (), s32[]{:S(2)}) async-start(), calls=%async_computation.8 | async-start | bytes 1327104 | tf_op jit(solution)/shard_map/all_gather | solution.py:370
  8.3 47.2 %copy-start.1 = (f32[768,96]{0,1:T(8,128)S(1)}, f32[768,96]{0,1:T(8,128)}, u32[]{:S(2)}) copy-start(f32[768,96]{0,1:T(8,128)} %param.16) | copy-start | bytes 884740
  8.6 47.6 %copy-start.6 = (f32[96]{0:T(128)S(1)}, f32[96]{0:T(128)}, u32[]{:S(2)}) copy-start(f32[96]{0:T(128)} %param.11) | copy-start | bytes 1156
  8.6 47.7 %copy-start.7 = (f32[96]{0:T(128)S(1)}, f32[96]{0:T(128)}, u32[]{:S(2)}) copy-start(f32[96]{0:T(128)} %param.10) | copy-start | bytes 1156
  8.6 47.7 %copy-start.8 = (u32[32]{0:T(128)S(1)}, u32[32]{0:T(128)}, u32[]{:S(2)}) copy-start(u32[32]{0:T(128)} %constant.26) | copy-start | bytes 388
  8.6 69.1 %copy-start.3 = (f32[3,8,64]{2,1,0:T(8,128)S(1)}, f32[3,8,64]{2,1,0:T(8,128)}, u32[]{:S(2)}) copy-start(f32[3,8,64]{2,1,0:T(8,128)} %param.13) | copy-start | bytes 18436
  9.6 101.0 %all-gather.13.cloned.1.call-start = ((), (), s32[]{:S(2)}) async-start(), calls=%async_computation.9 | async-start | bytes 5898240 | tf_op jit(solution)/shard_map/all_gather | solution.py:371
  54.7 81.6 %all-gather.15.cloned.1.call-start = ((), (), s32[]{:S(2)}) async-start(), calls=%async_computation.10 | async-start | bytes 1327104 | tf_op jit(solution)/shard_map/all_gather | solution.py:370
  55.4 123.5 %all-gather.19.cloned.1.call-start = ((), (), s32[]{:S(2)}) async-start(), calls=%async_computation.12 | async-start | bytes 1327104 | tf_op jit(solution)/shard_map/all_gather | solution.py:370
  56.2 143.0 %all-gather.23.cloned.1.call-start = ((), (), s32[]{:S(2)}) async-start(), calls=%async_computation.22 | async-start | bytes 1966080 | tf_op jit(solution)/shard_map/all_gather | solution.py:283
  128.3 109.8 %all-gather.17.cloned.1.call-start = ((), (), s32[]{:S(2)}) async-start(), calls=%async_computation.11 | async-start | bytes 5898240 | tf_op jit(solution)/shard_map/all_gather | solution.py:371
  136.3 140.8 %all-gather.21.cloned.1.call-start = ((), (), s32[]{:S(2)}) async-start(), calls=%async_computation.13 | async-start | bytes 5898240 | tf_op jit(solution)/shard_map/all_gather | solution.py:371
  178.9 155.7 %all-gather.25.cloned.1.call-start = ((), (), s32[]{:S(2)}) async-start(), calls=%async_computation.23 | async-start | bytes 1966080 | tf_op jit(solution)/shard_map/all_gather | solution.py:283
  314.8 70.2 %reduce-scatter.21.cloned.1.call-start = ((), (), s32[]{:S(2)}) async-start(), calls=%async_computation.20 | async-start | bytes 5898240 | tf_op jit(solution)/shard_map/reduce_scatter | solution.py:374
  315.5 119.6 %reduce-scatter.17.cloned.1.call-start = ((), (), s32[]{:S(2)}) async-start(), calls=%async_computation.18 | async-start | bytes 5898240 | tf_op jit(solution)/shard_map/reduce_scatter | solution.py:374
  316.1 169.4 %reduce-scatter.9.cloned.1.call-start = ((), (), s32[]{:S(2)}) async-start(), calls=%async_computation.14 | async-start | bytes 5898240 | tf_op jit(solution)/shard_map/reduce_scatter | solution.py:374
  365.4 160.2 %reduce-scatter.13.cloned.1.call-start = ((), (), s32[]{:S(2)}) async-start(), calls=%async_computation.16 | async-start | bytes 491520 | tf_op jit(solution)/shard_map/reduce_scatter | solution.py:394
  366.0 211.0 %reduce-scatter.23.cloned.1.call-start = ((), (), s32[]{:S(2)}) async-start(), calls=%async_computation.21 | async-start | bytes 1327104 | tf_op jit(solution)/shard_map/reduce_scatter | solution.py:375
  384.9 100.7 %copy-start.4 = (f32[1,768]{1,0:T(1,128)S(1)}, f32[1,768]{1,0:T(1,128)}, u32[]{:S(2)}) copy-start(f32[1,768]{1,0:T(1,128)} %get-tuple-element.46) | copy-start | bytes 9220
  384.9 100.7 %copy-start.5 = (f32[1,768]{1,0:T(1,128)S(1)}, f32[1,768]{1,0:T(1,128)}, u32[]{:S(2)}) copy-start(f32[1,768]{1,0:T(1,128)} %get-tuple-element.45) | copy-start | bytes 9220
  385.0 259.0 %reduce-scatter.19.cloned.1.call-start = ((), (), s32[]{:S(2)}) async-start(), calls=%async_computation.19 | async-start | bytes 1327104 | tf_op jit(solution)/shard_map/reduce_scatter | solution.py:375
  435.2 275.8 %reduce-scatter.11.cloned.1.call-start = ((), (), s32[]{:S(2)}) async-start(), calls=%async_computation.15 | async-start | bytes 1327104 | tf_op jit(solution)/shard_map/reduce_scatter | solution.py:375
  485.6 287.2 %reduce-scatter.15.cloned.1.call-start = ((), (), s32[]{:S(2)}) async-start(), calls=%async_computation.17 | async-start | bytes 110592 | tf_op jit(solution)/shard_map/reduce_scatter | solution.py:395
  (1 other events, 1.6 us)
Sparse Core Ops, SparseCore 0:
  10.8 43.8 all-gather.10
  56.2 36.1 all-gather.12
  95.1 41.1 all-gather.14
  138.9 39.9 all-gather.18
  180.9 18.3 all-gather.22
  200.6 37.4 all-gather.16
  239.7 37.4 all-gather.20
  314.9 19.6 all-gather.24
  337.1 47.7 reduce-scatter.20
  387.3 47.7 reduce-scatter.16
  437.7 47.7 reduce-scatter.8
  487.9 20.8 reduce-scatter.12
  512.1 64.8 reduce-scatter.22
  580.2 63.6 reduce-scatter.18
  647.2 63.7 reduce-scatter.10
  714.6 58.0 reduce-scatter.14

commit v2 on v1

--- a/solution.py
+++ b/solution.py
@@ -362,45 +362,455 @@
     return jnp.stack([query, key, grad[:, 2 * part : 3 * part]]), grad[:, 3 * part :].T
 
 
+MESH = pl.DeviceIdType.MESH
+LINE = 4
+
+
+class Place:
+    def __init__(self):
+        share, spot = lax.axis_index("dp"), lax.axis_index("tensor")
+        self.z, self.x = share // 2, lax.rem(share, 2)
+        self.y, self.core = spot // 2, lax.rem(spot, 2)
+        core = self.core
+        near = (lax.rem(self.x + 1 - core, 2), lax.rem(self.y + core, 2))
+        far = (lax.rem(self.x + core, 2), lax.rem(self.y + 1 - core, 2))
+        self.sides = [(self.x, self.y), near, far, (1 - self.x, 1 - self.y)]
+
+    def device(self, z, side, core):
+        x, y = self.sides[side]
+        return (z * 2 + x, y * 2 + core)
+
+    def right(self):
+        return self.device(self.z + 1, 0, self.core)
+
+    def left(self):
+        return self.device(self.z - 1, 0, self.core)
+
+    def near(self):
+        return self.device(self.z, 1, self.core)
+
+    def far(self):
+        return self.device(self.z, 2, self.core)
+
+    def twin(self):
+        return self.device(self.z, 0, 1 - self.core)
+
+    def meet(self):
+        barrier = pltpu.get_barrier_semaphore()
+
+        def greet(who):
+            pl.semaphore_signal(barrier, inc=1, device_id=who, device_id_type=MESH)
+
+        greet(self.near())
+        greet(self.far())
+        greet(self.twin())
+
+        @pl.when(self.z > 0)
+        def _():
+            greet(self.left())
+
+        @pl.when(self.z < LINE - 1)
+        def _():
+            greet(self.right())
+
+        ends = (self.z == 0) | (self.z == LINE - 1)
+
+        @pl.when(ends)
+        def _():
+            pl.semaphore_wait(barrier, 4)
+
+        @pl.when(jnp.logical_not(ends))
+        def _():
+            pl.semaphore_wait(barrier, 5)
+
+
+def gather_kernel(count, *refs):
+    blocks, full = refs[:count], refs[count : 2 * count]
+    send_sem, recv_sem, local_sem = refs[2 * count :]
+    place = Place()
+    width = blocks[0].shape[1]
+    used = [0] * count
+    pending = []
+
+    def slot(a, z, side, core):
+        share, spot = place.device(z, side, core)
+        return full[a].at[share, :, pl.ds(pl.multiple_of(spot * width, width), width)]
+
+    def arrival(a, z, side, core):
+        share, spot = place.device(z, side, core)
+        return recv_sem.at[a, share * 4 + spot]
+
+    def send(a, source, z, side, who, valid):
+        index = used[a]
+        used[a] += 1
+        copy = pltpu.make_async_remote_copy(
+            src_ref=source,
+            dst_ref=slot(a, z, side, place.core),
+            send_sem=send_sem.at[a, index],
+            recv_sem=arrival(a, z, side, place.core),
+            device_id=who,
+            device_id_type=MESH,
+        )
+        when(valid, copy.start)
+        pending.append((valid, copy))
+
+    def when(valid, action):
+        if valid is None:
+            action()
+        else:
+            pl.when(valid)(action)
+
+    def wait(a, z, side, core, valid):
+        here = slot(a, z, side, core)
+        copy = pltpu.make_async_remote_copy(
+            src_ref=here,
+            dst_ref=here,
+            send_sem=send_sem.at[a, 0],
+            recv_sem=arrival(a, z, side, core),
+            device_id=place.twin(),
+            device_id_type=MESH,
+        )
+        when(valid, copy.wait_recv)
+
+    place.meet()
+    local = []
+    for a in range(count):
+        keep = pltpu.make_async_copy(
+            blocks[a], slot(a, place.z, 0, place.core), local_sem.at[a]
+        )
+        keep.start()
+        local.append(keep)
+        send(a, blocks[a], place.z, 0, place.right(), place.z < LINE - 1)
+        send(a, blocks[a], place.z, 0, place.left(), place.z > 0)
+        send(a, blocks[a], place.z, 0, place.near(), None)
+        send(a, blocks[a], place.z, 0, place.far(), None)
+        send(a, blocks[a], place.z, 0, place.twin(), None)
+
+    def line_task(a, offset):
+        z = place.z + offset
+        valid = (z >= 0) & (z < LINE)
+        wait(a, z, 0, place.core, valid)
+        here = slot(a, z, 0, place.core)
+        if offset < 0:
+            send(a, here, z, 0, place.right(), valid & (place.z < LINE - 1))
+        else:
+            send(a, here, z, 0, place.left(), valid & (place.z > 0))
+        send(a, here, z, 0, place.near(), valid)
+        send(a, here, z, 0, place.far(), valid)
+        send(a, here, z, 0, place.twin(), valid)
+
+    def side_task(a, offset, side):
+        z = place.z + offset
+        valid = None if offset == 0 else (z >= 0) & (z < LINE)
+        wait(a, z, side, place.core, valid)
+        here = slot(a, z, side, place.core)
+        if side == 1:
+            send(a, here, z, side, place.far(), valid)
+        send(a, here, z, side, place.twin(), valid)
+
+    for hop in range(1, LINE + 2):
+        for a in range(count):
+            for side, delay in ((0, 0), (1, 1), (2, 1), (3, 2)):
+                reach = hop - delay
+                if reach < 0 or reach >= LINE or (side == 0 and reach == 0):
+                    continue
+                for offset in (0,) if reach == 0 else (-reach, reach):
+                    if side == 0:
+                        line_task(a, offset)
+                    else:
+                        side_task(a, offset, side)
+    for a in range(count):
+        for z in range(LINE):
+            for side in range(4):
+                wait(a, z, side, 1 - place.core, None)
+    for keep in local:
+        keep.wait()
+    for valid, copy in pending:
+        when(valid, copy.wait_send)
+
+
+def scatter_kernel(count, *refs):
+    grads, sums = refs[:count], refs[count : 2 * count]
+    rest = refs[2 * count :]
+    buffers = [rest[6 * a : 6 * a + 6] for a in range(count)]
+    send_sem, recv_sem, local_sem = rest[6 * count :]
+    place = Place()
+    width = sums[0].shape[1]
+    used = [0] * count
+    pending = []
+
+    def when(valid, action):
+        if valid is None:
+            action()
+        else:
+            pl.when(valid)(action)
+
+    def part(a, z, side, core):
+        share, spot = place.device(z, side, core)
+        return grads[a].at[share, :, pl.ds(pl.multiple_of(spot * width, width), width)]
+
+    def send(a, source, target, arrival, who, valid=None):
+        index = used[a]
+        used[a] += 1
+        copy = pltpu.make_async_remote_copy(
+            src_ref=source,
+            dst_ref=target,
+            send_sem=send_sem.at[a, index],
+            recv_sem=recv_sem.at[a, arrival],
+            device_id=who,
+            device_id_type=MESH,
+        )
+        when(valid, copy.start)
+        pending.append((valid, copy))
+
+    def wait(a, target, arrival, valid=None):
+        copy = pltpu.make_async_remote_copy(
+            src_ref=target,
+            dst_ref=target,
+            send_sem=send_sem.at[a, 0],
+            recv_sem=recv_sem.at[a, arrival],
+            device_id=place.twin(),
+            device_id_type=MESH,
+        )
+        when(valid, copy.wait_recv)
+
+    place.meet()
+    loads = {}
+    swap = (0, 2, 1, 3)
+    for a in range(count):
+        mine, twin = buffers[a][0], buffers[a][1]
+        for side in (3, 2, 1, 0):
+            for z in range(LINE):
+                index = side * LINE + z
+                send(
+                    a, part(a, z, swap[side], 1 - place.core), twin.at[index], index, place.twin()
+                )
+                load = pltpu.make_async_copy(
+                    part(a, z, side, place.core), mine.at[index], local_sem.at[a, index]
+                )
+                load.start()
+                loads[a, index] = load
+
+    def join(a, index):
+        mine, twin = buffers[a][0], buffers[a][1]
+        loads[a, index].wait()
+        wait(a, twin.at[index], index)
+        return mine[index].astype(single) + twin[index].astype(single)
+
+    def far_task(a):
+        mine, far = buffers[a][0], buffers[a][2]
+        for side, row in ((3, 1), (2, 0)):
+            for z in range(LINE):
+                index = side * LINE + z
+                mine[index] = join(a, index).astype(bfloat)
+                there = row * LINE + z
+                send(a, mine.at[index], far.at[there], 16 + there, place.far())
+
+    def near_task(a):
+        mine, far, near = buffers[a][0], buffers[a][2], buffers[a][3]
+        for z in range(LINE):
+            index = LINE + z
+            total = join(a, index)
+            wait(a, far.at[LINE + z], 16 + LINE + z)
+            mine[index] = (total + far[LINE + z].astype(single)).astype(bfloat)
+            send(a, mine.at[index], near.at[z], 24 + z, place.near())
+
+    def line_task(a):
+        mine, _, far, near, left, right = buffers[a]
+        for z in range(LINE):
+            total = join(a, z)
+            wait(a, far.at[z], 16 + z)
+            total = total + far[z].astype(single)
+            wait(a, near.at[z], 24 + z)
+            mine[z] = (total + near[z].astype(single)).astype(bfloat)
+
+            def onward(z, came, base, has, valid, who):
+                @pl.when(valid & has)
+                def _():
+                    wait(a, came.at[z], base + z)
+                    mine[z] = (mine[z].astype(single) + came[z].astype(single)).astype(bfloat)
+
+                send(a, mine.at[z], came.at[z], base + z, who, valid)
+
+            if z > 0:
+                onward(z, left, 28, place.z > 0, place.z < z, place.right())
+            if z < LINE - 1:
+                onward(z, right, 32, place.z < LINE - 1, place.z > z, place.left())
+
+    def last_task(a):
+        mine, _, _, _, left, right = buffers[a]
+        for z in range(LINE):
+
+            @pl.when(place.z == z)
+            def _(z=z):
+                total = mine[z].astype(single)
+                if z > 0:
+                    wait(a, left.at[z], 28 + z)
+                    total = total + left[z].astype(single)
+                if z < LINE - 1:
+                    wait(a, right.at[z], 32 + z)
+                    total = total + right[z].astype(single)
+                sums[a][...] = total
+
+    tasks = (far_task, near_task, line_task, last_task)
+    for wave in range(count + len(tasks) - 1):
+        for level in reversed(range(len(tasks))):
+            if 0 <= wave - level < count:
+                tasks[level](wave - level)
+    for valid, copy in pending:
+        when(valid, copy.wait_send)
+
+
+def gather_call(blocks, dp, groups):
+    count = len(blocks)
+    anywhere = pl.BlockSpec(memory_space=pl.ANY)
+    return pl.pallas_call(
+        functools.partial(gather_kernel, count),
+        out_shape=[
+            jax.ShapeDtypeStruct((dp, b.shape[0], groups * b.shape[1]), b.dtype) for b in blocks
+        ],
+        in_specs=[anywhere] * count,
+        out_specs=[anywhere] * count,
+        scratch_shapes=[
+            pltpu.SemaphoreType.DMA((count, 64)),
+            pltpu.SemaphoreType.DMA((count, dp * groups)),
+            pltpu.SemaphoreType.DMA((count,)),
+        ],
+        compiler_params=pltpu.CompilerParams(collective_id=0, has_side_effects=True),
+    )(*blocks)
+
+
+def scatter_call(grads, dp, groups):
+    count = len(grads)
+    width = grads[0].shape[2] // groups
+    slots = (16, 16, 8, 4, 4, 4)
+    return pl.pallas_call(
+        functools.partial(scatter_kernel, count),
+        out_shape=[jax.ShapeDtypeStruct((g.shape[1], width), single) for g in grads],
+        in_specs=[pl.BlockSpec(memory_space=pl.ANY)] * count,
+        out_specs=[pl.BlockSpec(memory_space=pltpu.VMEM)] * count,
+        scratch_shapes=[
+            pltpu.VMEM((slot, g.shape[1], width), bfloat) for g in grads for slot in slots
+        ]
+        + [
+            pltpu.SemaphoreType.DMA((count, 48)),
+            pltpu.SemaphoreType.DMA((count, 36)),
+            pltpu.SemaphoreType.DMA((count, 16)),
+        ],
+        compiler_params=pltpu.CompilerParams(
+            collective_id=1, has_side_effects=True, vmem_limit_bytes=LIMIT
+        ),
+    )(*grads)
+
+
+def kernel_gather(dp, groups, gain_one, gain_two, feature, square, up, down):
+    width = square.shape[1]
+    rows = gain_one.shape[0]
+    small = jnp.concatenate(
+        [feature.reshape(-1), gain_one, gain_two, jnp.zeros((width - 2 * rows,), bfloat)]
+    ).reshape(-1, width)
+    small = jnp.pad(small, ((0, 16 - small.shape[0]), (0, 0)))
+    square, up, down, small = gather_call([square, up, down, small], dp, groups)
+    full = [part.reshape(-1, groups * width) for part in (square, up, down)]
+    heads, piece, size = feature.shape
+    maps = small[:, :2].reshape(dp, 2, groups, width).transpose(2, 0, 1, 3)
+    maps = maps.reshape(groups, dp, heads, piece, size).transpose(0, 2, 1, 3, 4)
+    gains = small[:, 2, : 2 * rows]
+    return (
+        gains[:, :rows].reshape(1, -1),
+        gains[:, rows:].reshape(1, -1),
+        maps.reshape(groups * heads, dp * piece, size),
+        *full,
+    )
+
+
+def kernel_scatter(dp, groups, gain_one, gain_two, feature, square, up, down):
+    width = square.shape[1] // groups
+    heads, _, size = feature.shape
+    local = heads // groups
+    piece = feature.shape[1] // dp
+    maps = feature.reshape(groups, local, dp, piece, size).transpose(2, 0, 1, 3, 4)
+    maps = maps.reshape(dp, groups, 2, width).transpose(0, 2, 1, 3).reshape(dp, 2, -1)
+    rows = gain_one.shape[1] // dp
+    gains = jnp.concatenate([gain_one.reshape(dp, rows), gain_two.reshape(dp, rows)], axis=1)
+    gains = jnp.pad(gains, ((0, 0), (0, width - 2 * rows)))
+    gains = jnp.tile(gains, (1, groups))[:, None]
+    small = jnp.concatenate([maps, gains], axis=1).astype(bfloat)
+    small = jnp.pad(small, ((0, 0), (0, 13), (0, 0)))
+    full = [part.reshape(dp, -1, groups * width) for part in (up, down, square)]
+    up, down, square, small = scatter_call(full + [small], dp, groups)
+    return (
+        small[2, :rows],
+        small[2, rows : 2 * rows],
+        small[:2].reshape(local, piece, size),
+        square,
+        up,
+        down,
+    )
+
+
+def plain_gather(dp, groups, gain_one, gain_two, feature, square, up, down):
+    def gathered(block):
+        rows = lax.all_gather(block, "dp", axis=0, tiled=True)
+        return lax.all_gather(rows, "tensor", axis=1, tiled=True)
+
+    feature = lax.all_gather(feature, "dp", axis=1, tiled=True)
+    return (
+        lax.all_gather(gain_one, "dp", axis=0, tiled=True)[None],
+        lax.all_gather(gain_two, "dp", axis=0, tiled=True)[None],
+        lax.all_gather(feature, "tensor", axis=0, tiled=True),
+        gathered(square),
+        gathered(up),
+        gathered(down),
+    )
+
+
+def plain_scatter(dp, groups, gain_one, gain_two, feature, square, up, down):
+    def scattered(grad):
+        rows = lax.psum_scatter(grad, "tensor", scatter_dimension=1, tiled=True)
+        return lax.psum_scatter(rows, "dp", scatter_dimension=0, tiled=True).astype(single)
+
+    feature = lax.psum_scatter(feature, "tensor", scatter_dimension=0, tiled=True)
+    feature = lax.psum_scatter(feature, "dp", scatter_dimension=1, tiled=True)
+    gains = lax.psum(jnp.concatenate([gain_one[0], gain_two[0]]), ("tensor", "dp"))
+    rows = gain_one.shape[1] // dp
+    place = lax.axis_index("dp") * rows
+    return (
+        lax.dynamic_slice(gains, (place,), (rows,)),
+        lax.dynamic_slice(gains, (place + rows * dp,), (rows,)),
+        feature,
+        scattered(square),
+        scattered(up),
+        scattered(down),
+    )
+
+
 def per_device(
     groups, dp, tokens, gain_one, gain_two, qkv_weight, feature_weight, out_weight, up_weight,
     down_weight, cotangent,
 ):
-    def gathered(block):
-        rows = lax.all_gather(block, "dp", axis=0, tiled=True)
-        return lax.all_gather(rows, "tensor", axis=1, tiled=True)
-
-    def scattered(grad):
-        rows = lax.psum_scatter(grad, "tensor", scatter_dimension=1, tiled=True)
-        return lax.psum_scatter(rows, "dp", scatter_dimension=0, tiled=True).astype(single)
-
-    square = gathered(pack_square(qkv_weight.astype(bfloat), out_weight.astype(bfloat)))
-    up = gathered(up_weight.astype(bfloat))
-    down = gathered(down_weight.astype(bfloat).T)
-    feature = lax.all_gather(feature_weight.astype(bfloat), "dp", axis=1, tiled=True)
-    feature = lax.all_gather(feature, "tensor", axis=0, tiled=True)
-    gain_first = lax.all_gather(gain_one.astype(bfloat), "dp", axis=0, tiled=True)
-    gain_second = lax.all_gather(gain_two.astype(bfloat), "dp", axis=0, tiled=True)
+    own = dp == 2 * LINE and groups == 4
+    gather, scatter = (kernel_gather, kernel_scatter) if own else (plain_gather, plain_scatter)
+    gain_first, gain_second, feature, square, up, down = gather(
+        dp, groups,
+        gain_one.astype(bfloat), gain_two.astype(bfloat), feature_weight.astype(bfloat),
+        pack_square(qkv_weight.astype(bfloat), out_weight.astype(bfloat)),
+        up_weight.astype(bfloat), down_weight.astype(bfloat).T,
+    )
     (
         block_out, tokens_grad, gain_one_sum, gain_two_sum,
         square_grad, feature_grad, up_grad, down_grad,
     ) = compute(
-        groups, tokens, cotangent, gain_first.astype(single)[None], gain_second.astype(single)[None],
+        groups, tokens, cotangent, gain_first.astype(single), gain_second.astype(single),
         feature, square, up, down,
     )
-    qkv_grad, out_grad = unpack_square(scattered(square_grad))
-    up_out = scattered(up_grad)
-    down_out = scattered(down_grad).T
-    feature_out = lax.psum_scatter(feature_grad, "tensor", scatter_dimension=0, tiled=True)
-    feature_out = lax.psum_scatter(feature_out, "dp", scatter_dimension=1, tiled=True)
-    gains = lax.psum(jnp.concatenate([gain_one_sum[0], gain_two_sum[0]]), ("tensor", "dp"))
-    rows = gain_one.shape[0]
-    place = lax.axis_index("dp") * rows
-    gain_one_out = lax.dynamic_slice(gains, (place,), (rows,))
-    gain_two_out = lax.dynamic_slice(gains, (place + rows * dp,), (rows,))
+    gain_one_out, gain_two_out, feature_out, square_out, up_out, down_out = scatter(
+        dp, groups, gain_one_sum, gain_two_sum, feature_grad, square_grad, up_grad, down_grad
+    )
+    qkv_grad, out_grad = unpack_square(square_out)
     return (
         block_out, tokens_grad, gain_one_out, gain_two_out, qkv_grad, feature_out, out_grad,
-        up_out, down_out,
+        up_out, down_out.T,
     )
 
 

time: 780 us -> 343 us (0.44)
  waiting for transfers between devices: 558 us -> 38.8 us
  Pallas kernels: 94.8 us -> 261 us
  blocking collectives: 90.1 us -> 0 us
  local copies, waits for them, and re-layouts: 5.34 us -> 13.3 us
    reduce_scatter x8 -> x0, waiting for transfers between devices: 359 us -> none  [the longest x3 182 us: scattered(): lax.psum_scatter(rows, 'dp', scatter_dimension=0, tiled=True).astype(single)]
    pallas_call x0 -> x2, Pallas kernels: none -> 166 us  [the longest x1 95.7 us: scatter_call(): pl.pallas_call(functools.partial(scatter_kernel, count), out_shape=[jax.S...]
    all_gather x6 -> x0, waiting for transfers between devices: 159 us -> none  [the longest x3 95.4 us: gathered(): rows = lax.all_gather(block, 'dp', axis=0, tiled=True)]
    psum x1 -> x0, blocking collectives: 39.4 us -> none  [per_device(): lax.psum(jnp.concatenate([gain_one_sum[0], gain_two_sum[0]]), ('tensor',...]
    all_gather x2 -> x0, blocking collectives: 31.6 us -> none  [the longest x1 26 us: per_device(): lax.all_gather(feature_weight.astype(bfloat), 'dp', axis=1, tiled=True)]
    unnamed x1 -> x0, blocking collectives: 19.1 us -> none
  transfers between devices with their start and end apart: 16 -> 2, of which waited for: 14 -> 2; matrix products, arithmetic and copies ran while one was open for 2% -> 0% of each run, Pallas kernels for 7% -> 0%
where the time goes in v2:
time: 343 us
  Pallas kernels  261 us (76%)
  waiting for transfers between devices  38.8 us (11%)
  other arithmetic  15.6 us (5%)
  between operations  14.3 us (4%)
  local copies, waits for them, and re-layouts  13.3 us (4%)
    pallas_call x1, Pallas kernels, scatter_call(): pl.pallas_call(functools.partial(scatter_kernel, count), out_shape=[jax.S...  95.7 us
    pallas_call x5, Pallas kernels, stage(): pl.pallas_call(kernel, grid=(groups,), in_specs=[kinds[kind](array, group...  94.6 us
    pallas_call x1, Pallas kernels, gather_call(): pl.pallas_call(functools.partial(gather_kernel, count), out_shape=[jax.Sh...  70.2 us
    all_gather x2, waiting for transfers between devices, state_before(): every = lax.all_gather(totals, 'tensor', axis=0)  38.8 us
  transfers between devices with their start and end apart: 2, of which 2 were waited for; matrix products, arithmetic and copies ran while one was open for 0% of the time, Pallas kernels for 0%

profile of v2, /device:TPU:0, one launch (start us, length us, event | category | flops | bytes accessed | tf_op | source)
XLA Modules:
  0.0 342.8 jit_solution(13510438412150542200)
XLA Ops:
  10.1 1.0 copy.39
  11.1 1.0 convert_element_type.50
  13.9 0.7 pad_maximum_fusion.1.refs_0_
  14.6 70.2 %shard_map.160 = (bf16[8,96,3072]{2,1,0:T(8,128)(2,1)}, bf16[8,96,3072]{2,1,0:T(8,128)(2,1)}, bf16[8,96,3072]{2,1,0:T(8,128)(2,1)}, bf16[8,16,3072]{2,1,0:T(8,128)(2,1)}) custom-call(bf16[96,768]{1,0:T(8,128)(2,1)} %pad_maximum_fusion.1.refs_0_, bf16[96,768]{1,0:T(8,128)(2,1)} %convert_element_type.52.refs_1_, bf16[96,768]{1,0:T(8,128)(2,1)} %convert_bitcast_fusion.refs_2_, ...), custom_call_target="tpu_custom_call" | custom-call | tf_op jit(solution)/shard_map/pallas_call | solution.py:667
  84.9 0.8 slice.48
  85.6 1.1 slice.51
  87.8 1.2 maximum_maximum_fusion.f_ref
  89.1 17.7 %shard_map.161 = (bf16[512,768]{1,0:T(8,128)(2,1)}, bf16[512,1536]{1,0:T(8,128)(2,1)}, bf16[512,3072]{1,0:T(8,128)(2,1)}, bf16[512,1536]{1,0:T(8,128)(2,1)}, bf16[12,128,128]{2,1,0:T(8,128)(2,1)}) custom-call(bf16[512,768]{1,0:T(8,128)(2,1)} %x_ref.5, f32[1,768]{1,0:T(1,128)} %reshape.145.gain_ref, bf16[768,3072]{1,0:T(8,128)(2,1)} %bitcast.53, ...), custom_call_target="tpu_custom_call" | custom-call | tf_op jit(solution)/shard_map/pallas_call | solution.py:266
  107.7 19.1 %all-gather.5.cloned.1.call-done = bf16[48,128,128]{2,1,0:T(8,128)(2,1)} async-done(((bf16[12,128,128]{2,1,0:T(8,128)(2,1)}), bf16[48,128,128]{2,1,0:T(8,128)(2,1)}) %all-gather.5.cloned.1.call-update) | async-done | bytes 1572880 | tf_op jit(solution)/shard_map/all_gather | solution.py:283
  126.8 2.7 fusion.1.state_ref
  129.5 11.0 %shard_map.162 = (bf16[4,512,192]{2,1,0:T(8,128)(2,1)}, f32[4,512,192]{2,1,0:T(8,128)}, f32[512,768]{1,0:T(8,128)}, bf16[512,768]{1,0:T(8,128)(2,1)}) custom-call(bf16[512,768]{1,0:T(8,128)(2,1)} %x_ref.5, f32[1,768]{1,0:T(1,128)} %reshape.144.gain_ref, bf16[768,3072]{1,0:T(8,128)(2,1)} %bitcast.54, bf16[512,3072]{1,0:T(8,128)(2,1)} %get-tuple-element.40.phi_ref, ...), custom_call_target="tpu_custom_call" | custom-call | tf_op jit(solution)/shard_map/pallas_call | solution.py:266
  140.5 24.0 %shard_map.163 = (f32[512,768]{1,0:T(8,128)}, f32[512,768]{1,0:T(8,128)}, bf16[512,768]{1,0:T(8,128)(2,1)}, f32[1,768]{1,0:T(1,128)}, bf16[768,3072]{1,0:T(8,128)(2,1)}, /*index=5*/bf16[768,3072]{1,0:T(8,128)(2,1)}) custom-call(f32[512,768]{1,0:T(8,128)} %get-tuple-element.43.middle_ref, f32[1,768]{1,0:T(1,128)} %reshape.144.gain_ref, ...), custom_call_target="tpu_custom_call" | custom-call | tf_op jit(solution)/shard_map/pallas_call | solution.py:266
  164.6 13.4 %shard_map.164 = (bf16[512,1536]{1,0:T(8,128)(2,1)}, bf16[12,128,128]{2,1,0:T(8,128)(2,1)}) custom-call(bf16[512,768]{1,0:T(8,128)(2,1)} %get-tuple-element.50.branch_ref, bf16[768,3072]{1,0:T(8,128)(2,1)} %bitcast.55, bf16[4,512,192]{2,1,0:T(8,128)(2,1)} %get-tuple-element.51.att_ref, f32[4,512,192]{2,1,0:T(8,128)} %get-tuple-element.53.inv_ref, ...), custom_call_target="tpu_custom_call" | custom-call | tf_op jit(solution)/shard_map/pallas_call | solution.py:266
  178.2 19.6 %all-gather.7.cloned.1.call-done = bf16[48,128,128]{2,1,0:T(8,128)(2,1)} async-done(((bf16[12,128,128]{2,1,0:T(8,128)(2,1)}), bf16[48,128,128]{2,1,0:T(8,128)(2,1)}) %all-gather.7.cloned.1.call-update) | async-done | bytes 1572880 | tf_op jit(solution)/shard_map/all_gather | solution.py:283
  197.8 2.7 fusion.later_ref
  200.5 28.4 %shard_map.165 = (f32[512,768]{1,0:T(8,128)}, f32[1,768]{1,0:T(1,128)}, bf16[768,3072]{1,0:T(8,128)(2,1)}, f32[12,64,64]{2,1,0:T(8,128)}) custom-call(bf16[512,768]{1,0:T(8,128)(2,1)} %x_ref.5, f32[1,768]{1,0:T(1,128)} %reshape.145.gain_ref, bf16[512,768]{1,0:T(8,128)(2,1)} %get-tuple-element.48.normed_ref, f32[512,768]{1,0:T(8,128)} %get-tuple-element.49.dmid_ref, ...), custom_call_target="tpu_custom_call" | custom-call | tf_op jit(solution)/shard_map/pallas_call | solution.py:266
  229.8 1.0 convert.15
  231.0 1.1 fusion.4.refs_3_
  232.2 95.7 %shard_map.166 = (f32[96,768]{1,0:T(8,128)}, f32[96,768]{1,0:T(8,128)}, f32[96,768]{1,0:T(8,128)}, f32[16,768]{1,0:T(8,128)}) custom-call(bf16[8,96,3072]{2,1,0:T(8,128)(2,1)} %bitcast.57, bf16[8,96,3072]{2,1,0:T(8,128)(2,1)} %bitcast.58, bf16[8,96,3072]{2,1,0:T(8,128)(2,1)} %bitcast.59, bf16[8,16,3072]{2,1,0:T(8,128)(2,1)} %fusion.4.refs_3_), custom_call_target="tpu_custom_call" | custom-call | tf_op jit(solution)/shard_map/pallas_call | solution.py:687
  327.9 1.3 slice_bitcast_fusion.3
  329.2 0.7 slice.58
  330.0 1.0 slice.54
  330.9 1.1 slice_bitcast_fusion
  332.7 0.7 copy.48
  (58 shorter events, 11.1 us)
Async XLA Ops:
  7.2 5.4 %copy-start = (f32[96,768]{1,0:T(8,128)S(1)}, f32[96,768]{1,0:T(8,128)}, u32[]{:S(2)}) copy-start(f32[96,768]{1,0:T(8,128)} %param.15) | copy-start | bytes 884740
  7.2 6.0 %copy-start.1 = (f32[768,96]{0,1:T(8,128)S(1)}, f32[768,96]{0,1:T(8,128)}, u32[]{:S(2)}) copy-start(f32[768,96]{0,1:T(8,128)} %param.16) | copy-start | bytes 884740
  7.2 119.6 %all-gather.5.cloned.1.call-start = ((), (), s32[]{:S(2)}) async-start(), calls=%async_computation | async-start | bytes 1966080 | tf_op jit(solution)/shard_map/all_gather | solution.py:283
  106.8 91.0 %all-gather.7.cloned.1.call-start = ((), (), s32[]{:S(2)}) async-start(), calls=%async_computation.1 | async-start | bytes 1966080 | tf_op jit(solution)/shard_map/all_gather | solution.py:283
  164.6 13.5 %copy-start.4 = (f32[1,768]{1,0:T(1,128)S(1)}, f32[1,768]{1,0:T(1,128)}, u32[]{:S(2)}) copy-start(f32[1,768]{1,0:T(1,128)} %get-tuple-element.62) | copy-start | bytes 9220
  327.9 6.6 %copy-start.3 = (f32[96,768]{1,0:T(8,128)S(1)}, f32[96,768]{1,0:T(8,128)}, u32[]{:S(2)}) copy-start(f32[96,768]{1,0:T(8,128)} %get-tuple-element.121) | copy-start | bytes 884740
  330.0 5.2 %copy-start.2 = (f32[96,768]{1,0:T(8,128)S(1)}, f32[96,768]{1,0:T(8,128)}, u32[]{:S(2)}) copy-start(f32[96,768]{1,0:T(8,128)} %get-tuple-element.66) | copy-start | bytes 884740
Sparse Core Ops, SparseCore 0:
  106.9 19.8 all-gather.4
  178.2 19.6 all-gather.6
